TPU v7x, 256 devices: a whole 4x4x8 slice. The times are simulated.
256 devices in a mesh: expert: 64 (over y, z, core), gate: 4 (over x).
Axes of the slice: x: 4, y: 4, z: 8, core: 2. Of those that a mesh axis runs over, the one named last changes fastest.
Arguments:
- samples: bfloat16 [49152, 4096], P('expert', 'gate'), may hold values from -4 to 4
- gate_weight: bfloat16 [4096, 256], P('gate'), may hold values from -1 to 1
- expert_ids: int32 [49152, 2], P('expert'), may hold values from 0 to 255, all different within a row; in each aligned block of 768 rows (0 to 767, 768 to 1535, ...) at most 12 rows name the same one
- pad_mask: int32 [49152], P('expert'), may hold values 0 or 1
- up_weight: bfloat16 [256, 4096, 1024], P(('expert', 'gate')), may hold values from -0.09375 to 0.09375
- down_weight: bfloat16 [256, 1024, 1024], P(('expert', 'gate')), may hold values from -0.1875 to 0.1875
Outputs:
- combined: bfloat16 [49152, 1024], P('expert', 'gate')
Inputs may be any that keep to these rules, and one draw needn't show every extreme that they name: `expert_ids`: each sample names two different experts; among the 768 samples of one index of expert no expert is named more than 12 times, a bound that some block reaches.
All inputs are finite; a program needn't handle non-finite values. No bound on the sum of `pad_mask` on one device may be relied on, other than what follows from the above.
Results may differ from a plain program's by a relative error of at most 0.0057.
Values may be sent and summed in bfloat16 or wider, within the bound.
A program may use at most 128 MiB of HBM per device.

v0:
```python
import jax
import jax.numpy as jnp
from jax import lax
from jax.sharding import PartitionSpec as P


def cut_along(shard, dim, peers):
    shape = shard.shape
    parts = shard.reshape(*shape[:dim], peers, shape[dim] // peers, *shape[dim + 1 :])
    return jnp.moveaxis(parts, dim, 0)


def sent_and_summed(shard, axis, dim):
    peers = lax.axis_size(axis)
    parts = lax.all_to_all(cut_along(shard, dim, peers), axis, 0, 0, tiled=True)
    return jnp.sum(parts, axis=0)


def in_order(parts, dim):
    parts = jnp.moveaxis(parts, 0, dim)
    shape = parts.shape
    return parts.reshape(*shape[:dim], shape[dim] * shape[dim + 1], *shape[dim + 2 :])


def joined_exchange(shard, axis, axes, splits, concats):
    sizes = [lax.axis_size(a) for a in axes]
    parts = cut_along(shard, splits[0], sizes[0])
    parts = jnp.moveaxis(cut_along(parts, splits[1] + 1, sizes[1]), 0, 1)
    inside = parts.shape[2:]
    parts = parts.reshape(-1, *inside)
    parts = lax.all_to_all(parts, axis, split_axis=0, concat_axis=0, tiled=True)
    parts = in_order(parts.reshape(*sizes, *inside), concats[0] + 1)
    return in_order(parts, concats[1])


def joined(shard, axis, combine):
    everything = jax.tree.map(lambda part: lax.all_gather(part, axis), shard)
    leading = jax.tree.map(lambda part: part[0], everything)

    def step(k, so_far):
        return combine(so_far, jax.tree.map(lambda part: part[k], everything))

    return lax.fori_loop(1, lax.axis_size(axis), step, leading)


def combine_parts(first, second):
    row_top = jnp.maximum(first[0], second[0])
    left_scale = jnp.exp(first[0] - row_top)
    right_scale = jnp.exp(second[0] - row_top)
    row_total = first[1] * left_scale + second[1] * right_scale
    chosen = first[2] * left_scale[None, :] + second[2] * right_scale[None, :]
    return (row_top, row_total, chosen)


def per_device(samples, gate_weight, expert_ids, pad_mask, up_weight, down_weight):
    row_count = samples.shape[0]
    feature_share = samples.shape[1]
    group_count = lax.axis_size("expert")
    gate_count = lax.axis_size("gate")
    expert_count = group_count * gate_count
    capacity = 4 * row_count // expert_count
    col_count = expert_count // gate_count
    gate_index = lax.axis_index("gate")
    logits_t = sent_and_summed(
        lax.dot_general(
            gate_weight, samples, (((0,), (1,)), ((), ())), preferred_element_type=jnp.float32
        ),
        "gate",
        0,
    )
    flat_ids = expert_ids.reshape(-1)
    onehot = (flat_ids[:, None] == jnp.arange(expert_count, dtype=jnp.int32)[None, :]).astype(
        jnp.int32
    )
    slot_rank = jnp.sum(onehot * (jnp.cumsum(onehot, axis=0) - 1), axis=1)
    position = flat_ids * capacity + slot_rank
    row_index = jnp.repeat(jnp.arange(row_count, dtype=jnp.int32), 2)
    owners = jnp.full((expert_count * capacity,), row_count, jnp.int32).at[position].set(row_index)
    padded = jnp.concatenate([samples, jnp.zeros((1, feature_share), samples.dtype)], axis=0)
    outgoing = padded[owners].reshape(group_count, gate_count, capacity, feature_share)
    incoming = joined_exchange(outgoing, ("expert", "gate"), ("expert", "gate"), (0, 1), (0, 3))
    slot_rows = incoming.reshape(group_count * capacity, feature_share * gate_count)
    hidden = jnp.dot(slot_rows, up_weight[0], preferred_element_type=jnp.float32)
    active = jnp.maximum(hidden, 0.0).astype(jnp.bfloat16)
    expert_out = jnp.dot(active, down_weight[0], preferred_element_type=jnp.float32).astype(
        jnp.bfloat16
    )
    out_share = expert_out.shape[1] // gate_count
    outbound = expert_out.reshape(group_count, 1, 1, capacity, gate_count, out_share)
    returned = joined_exchange(outbound, ("expert", "gate"), ("expert", "gate"), (0, 4), (1, 2))
    returned = returned.reshape(expert_count * capacity, out_share)
    offset = expert_ids - gate_index * col_count
    inside = ((offset >= 0) & (offset < col_count)).T
    chosen = jnp.take_along_axis(logits_t, jnp.clip(offset, 0, col_count - 1).T, axis=0)
    local_top = jnp.max(logits_t, axis=0)
    local_total = jnp.sum(jnp.exp(logits_t - local_top[None, :]), axis=0)
    local_chosen = jnp.where(inside, jnp.exp(chosen - local_top[None, :]), 0.0)
    row_top, row_total, numerator = joined(
        (local_top, local_total, local_chosen), "gate", combine_parts
    )
    factor = expert_count * numerator / row_total[None, :] * pad_mask.astype(jnp.float32)[None, :]
    picked = returned[position].astype(jnp.float32).reshape(row_count, 2, out_share)
    mixed = factor[0][:, None] * picked[:, 0, :] + factor[1][:, None] * picked[:, 1, :]
    return mixed.astype(jnp.bfloat16)


def solution(mesh):
    placed = (
        P("expert", "gate"),
        P("gate", None),
        P("expert", None),
        P("expert"),
        P(("expert", "gate"), None, None),
        P(("expert", "gate"), None, None),
    )
    return jax.shard_map(
        per_device, mesh=mesh, in_specs=placed, out_specs=P("expert", "gate"), check_vma=False
    )
```

profile of v0, /device:TPU:1, one launch (start us, length us, event | category | flops | bytes accessed | tf_op | source)
XLA Modules:
  0.0 386.3 jit_solution(15585630266988360881)
XLA Ops:
  0.0 0.8 broadcast_multiply_fusion
  0.8 0.9 copy.20
  2.7 0.3 fusion.5
  3.1 1.3 copy-done.1
  4.5 1.8 add_add_fusion
  6.3 2.1 copy.23
  8.6 1.9 fusion.12
  10.6 6.2 %scatter_custom_fusion = s32[3072]{0:T(1024)S(1)} fusion(s32[1536]{0:T(1024)S(1)} %fusion.19, s32[1536]{0:T(1024)S(1)} %reshape.125, s32[]{:T(128)} %constant.82.clone.1), kind=kCustom, calls=%fused_computation.48 | custom fusion | bytes 12292 | tf_op jit(solution)/shard_map/scatter | solution.py:78
  16.8 2.7 concatenate.3
  19.5 17.6 %gather_fusion = bf16[3072,1024]{1,0:T(8,128)(2,1)} fusion(bf16[769,1024]{1,0:T(8,128)(2,1)} %concatenate.3, s32[3072]{0:T(1024)S(1)} %fusion.18), kind=kCustom, calls=%fused_computation | custom fusion | bytes 12595200 | tf_op jit(solution)/shard_map/gather | solution.py:80
  37.0 10.6 %reshape_transpose_transpose_reshape_reshape_reshape.3 = bf16[256,1,1,12,1024]{4,3,0,2,1:T(8,128)(2,1)} reshape(bf16[3072,1024]{1,0:T(8,128)(2,1)} %gather_fusion) | data formatting | bytes 12582912 | tf_op jit(solution)/shard_map/reshape;transpose;transpose;reshape;reshape;reshape | solution.py:30
  47.6 16.6 %all-to-all-start.1 = ((bf16[256,1,1,12,1024]{4,3,2,1,0:T(8,128)(2,1)}), bf16[256,1,1,12,1024]{4,3,2,1,0:T(8,128)(2,1)}, u32[]{:S(2)}, u32[]{:S(2)}) async-start(bf16[256,1,1,12,1024]{4,3,2,1,0:T(8,128)(2,1)} %bitcast.100), calls=%async_computation.1 | async-start | bytes 16777216 | tf_op jit(solution)/shard_map/all_to_all | solution.py:31
  64.3 2.9 fusion.25
  67.2 185.7 %all-to-all-done.1 = bf16[256,1,1,12,1024]{4,3,2,1,0:T(8,128)(2,1)} async-done(((bf16[256,1,1,12,1024]{4,3,2,1,0:T(8,128)(2,1)}), bf16[256,1,1,12,1024]{4,3,2,1,0:T(8,128)(2,1)}, u32[]{:S(2)}, u32[]{:S(2)}) %all-to-all-start.1) | async-done | bytes 6291488 | tf_op jit(solution)/shard_map/all_to_all | solution.py:31
  252.9 3.7 all-to-all-start
  256.6 18.9 %copy.25 = bf16[64,4,1,1,12,1024]{5,1,4,0,3,2:T(4,128)(2,1)} copy(bf16[64,4,1,1,12,1024]{5,4,1,0,3,2:T(8,128)(2,1)} %bitcast.11) | data formatting | bytes 12582912 | tf_op jit(solution)/shard_map/reshape | solution.py:32
  275.4 9.5 %copy.35 = bf16[96,8,4,1024]{3,1,2,0:T(8,128)(2,1)} copy(bf16[96,8,4,1024]{3,2,1,0:T(4,128)(2,1)} %bitcast.101) | data formatting | bytes 12582912
  285.0 14.6 %fusion.9 = bf16[768,1024]{1,0:T(8,128)(2,1)} fusion(bf16[1,1024,1024]{2,1,0:T(8,128)(2,1)S(1)} %copy-done, bf16[768,4096]{1,0:T(8,128)(2,1)} %bitcast.103, bf16[1,4096,1024]{2,1,0:T(8,128)(2,1)} %param.12), kind=kOutput, calls=%fused_computation.20 | convolution fusion | flops 8055422976 | bytes 18350080 | tf_op jit(solution)/shard_map/dot_general | solution.py:85
  299.6 4.1 %reshape_reshape_reshape.3 = bf16[64,1,1,1,12,4,1,256]{7,5,4,0,6,3,2,1:T(4,128)(2,1)} reshape(bf16[768,1024]{1,0:T(8,128)(2,1)} %fusion.9) | data formatting | bytes 3145728 | tf_op jit(solution)/shard_map/reshape;reshape;reshape | solution.py:9
  303.7 2.1 copy.51
  305.8 2.9 copy.30
  308.7 7.9 %all-to-all-start.2 = ((bf16[256,1,1,1,12,1,256]{6,4,5,3,2,1,0:T(8,128)(2,1)}), bf16[256,1,1,1,12,1,256]{6,4,5,3,2,1,0:T(8,128)(2,1)}, u32[]{:S(2)}, u32[]{:S(2)}) async-start(bf16[256,1,1,1,12,1,256]{6,4,5,3,2,1,0:T(8,128)(2,1)} %bitcast.102), calls=%async_computation.2 | async-start | bytes 4194304 | tf_op jit(solution)/shard_map/all_to_all | solution.py:31
  316.8 12.7 %gather_fusion.2 = f32[1536]{0:T(1024)S(1)} fusion(f32[64,768]{1,0:T(8,128)S(1)} %reduce_sum.29, s32[1536]{0:T(1024)S(1)} %reshape.115), kind=kCustom, calls=%fused_computation.2 | custom fusion | bytes 24576 | tf_op jit(solution)/shard_map/jit(take_along_axis)/gather | solution.py:94
  329.6 10.6 %all-gather.3 = f32[4,1,768]{2,1,0:T(1,128)S(1)} all-gather(f32[1,1,768]{2,1,0:T(1,128)S(1)} %reshape.144), channel_id=2, replica_groups=mesh['expert'=64,'gate'=4] {'gate'}, dimensions={0}, use_global_device_ids=true | all-gather | bytes 15360 | tf_op jit(solution)/shard_map/all_gather | solution.py:37
  340.2 10.1 %all-gather.4 = f32[4,1,768]{2,1,0:T(1,128)S(1)} all-gather(f32[1,1,768]{2,1,0:T(1,128)S(1)} %reshape.146), channel_id=3, replica_groups=mesh['expert'=64,'gate'=4] {'gate'}, dimensions={0}, use_global_device_ids=true | all-gather | bytes 15360 | tf_op jit(solution)/shard_map/all_gather | solution.py:37
  350.3 10.3 %all-gather.5 = f32[4,2,768]{2,1,0:T(2,128)S(1)} all-gather(f32[1,2,768]{2,1,0:T(2,128)S(1)} %fusion.21), channel_id=4, replica_groups=mesh['expert'=64,'gate'=4] {'gate'}, dimensions={0}, use_global_device_ids=true | all-gather | bytes 30720 | tf_op jit(solution)/shard_map/all_gather | solution.py:37
  360.9 9.8 %all-to-all-done.2 = bf16[256,1,1,1,12,1,256]{6,4,5,3,2,1,0:T(8,128)(2,1)} async-done(((bf16[256,1,1,1,12,1,256]{6,4,5,3,2,1,0:T(8,128)(2,1)}), bf16[256,1,1,1,12,1,256]{6,4,5,3,2,1,0:T(8,128)(2,1)}, u32[]{:S(2)}, u32[]{:S(2)}) %all-to-all-start.2) | async-done | bytes 1572896 | tf_op jit(solution)/shard_map/all_to_all | solution.py:31
  370.7 3.7 reshape_reshape.7
  374.4 5.3 %gather_fusion.1 = bf16[1536,256]{1,0:T(8,128)(2,1)S(1)} fusion(bf16[3072,256]{1,0:T(8,128)(2,1)} %reshape_reshape.7, s32[2048]{0:T(1024)S(1)} %pad_clamp_fusion), kind=kCustom, calls=%fused_computation.1 | custom fusion | bytes 1579008 | tf_op jit(solution)/shard_map/gather | solution.py:102
  379.7 1.9 reshape.98
  381.6 3.3 fusion.24
  384.8 1.0 fusion.16
  (49 shorter events, 2.1 us)
Async XLA Ops:
  0.0 285.0 %copy-start = (bf16[1,1024,1024]{2,1,0:T(8,128)(2,1)S(1)}, bf16[1,1024,1024]{2,1,0:T(8,128)(2,1)}, u32[]{:S(2)}) copy-start(bf16[1,1024,1024]{2,1,0:T(8,128)(2,1)} %param.13) | copy-start | bytes 6291460
  3.1 1.4 copy-start.1
  47.6 16.7 %copy-start.2 = (bf16[1024,256]{1,0:T(8,128)(2,1)S(1)}, bf16[1024,256]{1,0:T(8,128)(2,1)}, u32[]{:S(2)}) copy-start(bf16[1024,256]{1,0:T(8,128)(2,1)} %param.9) | copy-start | bytes 1572868
  47.6 205.3 %all-to-all-start.1 = ((bf16[256,1,1,12,1024]{4,3,2,1,0:T(8,128)(2,1)}), bf16[256,1,1,12,1024]{4,3,2,1,0:T(8,128)(2,1)}, u32[]{:S(2)}, u32[]{:S(2)}) async-start(bf16[256,1,1,12,1024]{4,3,2,1,0:T(8,128)(2,1)} %bitcast.100), calls=%async_computation.1 | async-start | bytes 16777216 | tf_op jit(solution)/shard_map/all_to_all | solution.py:31
  252.9 55.8 %all-to-all-start = ((f32[4,64,768]{2,1,0:T(8,128)}), f32[4,64,768]{2,1,0:T(8,128)S(1)}, u32[]{:S(2)}, u32[]{:S(2)}) async-start(f32[4,64,768]{2,1,0:T(8,128)} %bitcast.105), calls=%async_computation | async-start | bytes 1572864 | tf_op jit(solution)/shard_map/all_to_all | solution.py:15
  308.7 7.9 %copy-start.3 = (s32[768,2]{0,1:T(2,128)S(1)}, s32[768,2]{0,1:T(2,128)}, u32[]{:S(2)}) copy-start(s32[768,2]{0,1:T(2,128)} %param.10) | copy-start | bytes 18436
  308.7 8.0 %copy-start.4 = (s32[768]{0:T(1024)S(1)}, s32[768]{0:T(1024)}, u32[]{:S(2)}) copy-start(s32[768]{0:T(1024)} %param.11) | copy-start | bytes 9220
  308.7 62.0 %all-to-all-start.2 = ((bf16[256,1,1,1,12,1,256]{6,4,5,3,2,1,0:T(8,128)(2,1)}), bf16[256,1,1,1,12,1,256]{6,4,5,3,2,1,0:T(8,128)(2,1)}, u32[]{:S(2)}, u32[]{:S(2)}) async-start(bf16[256,1,1,1,12,1,256]{6,4,5,3,2,1,0:T(8,128)(2,1)} %bitcast.102), calls=%async_computation.2 | async-start | bytes 4194304 | tf_op jit(solution)/shard_map/all_to_all | solution.py:31
where the time goes:
time: 393 us; the launch traced here: 386 us
  waiting for transfers between devices  195 us (50%)
  local copies, waits for them, and re-layouts  107 us (27%)
  blocking collectives  30.9 us (8%)
  starting transfers between devices  28.2 us (7%)
  matrix products  17.5 us (4%)
  other arithmetic  6.29 us (2%)
    all_to_all x2, waiting for transfers between devices, joined_exchange(): parts = lax.all_to_all(parts, axis, split_axis=0, concat_axis=0, tiled=True)  195 us
    all_gather x3, blocking collectives, joined(): everything = jax.tree.map(lambda part: lax.all_gather(part, axis), shard)  30.9 us
    all_to_all x2, starting transfers between devices, joined_exchange(): parts = lax.all_to_all(parts, axis, split_axis=0, concat_axis=0, tiled=True)  24.6 us
    reshape x1, local copies, waits for them, and re-layouts, joined_exchange(): parts = in_order(parts.reshape(*sizes, *inside), concats[0] + 1)  18.9 us
    gather x1, local copies, waits for them, and re-layouts, per_device(): padded[owners].reshape(group_count, gate_count, capacity, feature_share)  17.6 us
    dot_general x1, matrix products, per_device(): jnp.dot(active, down_weight[0], preferred_element_type=jnp.float32)  14.6 us
    gather x3, local copies, waits for them, and re-layouts, per_device(): jnp.take_along_axis(logits_t, jnp.clip(offset, 0, col_count - 1).T, axis=0)  12.7 us
    unnamed x16, local copies, waits for them, and re-layouts  11.8 us
  transfers between devices with their start and end apart: 3, of which 2 were waited for; matrix products, arithmetic and copies ran while one was open for 18% of the time, Pallas kernels for 0%

commit v1 on v0

v1 whole, which is shorter than its diff:
```python
import functools

import jax
import jax.numpy as jnp
from jax import lax
from jax.experimental import pallas as pl
from jax.experimental.pallas import tpu as pltpu
from jax.sharding import PartitionSpec as P

MESH = pl.DeviceIdType.MESH
Y, Z, C, X = 4, 8, 2, 4
CAP = 12
F32, BF16, I32 = jnp.float32, jnp.bfloat16, jnp.int32
EXACT = dict(preferred_element_type=F32)


def iota(shape, dim):
    return lax.broadcasted_iota(I32, shape, dim)


def div(v, n):
    return lax.shift_right_logical(v * (-(-(1 << 17) // n)), 17)


def as_mask(cond):
    return jnp.where(cond, 1.0, 0.0).astype(BF16)


def kernel(
    samples, gate, ids, mask, up, down, out,
    sv, gv, w1, w2, near, hop, far, last,
    sb0, sb1, sb2, sb3, sb4, xb0, xb1, xb2, xb3, xb4,
    ob0, ob1, ob2, ob3, ob4, rb0, rb1, rb2, rb3, rb4,
    zs, zr, posb, rowb, pick, pickr, cols, lpart, lrecv, fac, act, acc,
    wsem, ssem, hsend, hrecv, isend, irecv, rsend, rrecv, zsend, zrecv, msend, mrecv,
):
    sb, xb = (sb0, sb1, sb2, sb3, sb4), (xb0, xb1, xb2, xb3, xb4)
    ob, rb = (ob0, ob1, ob2, ob3, ob4), (rb0, rb1, rb2, rb3, rb4)
    width = (16, 24, 24, 24, 16)
    ne = lax.axis_index("expert")
    x = lax.axis_index("gate")
    y, z, c = ne // (Z * C), (ne // C) % Z, ne % C
    half = Y * C * X * CAP // 2
    nf = sv.shape[0]
    rows = sv.shape[1]
    wide = sv.shape[2]
    share = rows // X

    def at_z(d):
        return (y * Z + (z + d) % Z) * C + c, x

    def in_plane(k):
        dy, dc, dx = k // (C * X), (k // X) % C, k % X
        y2, c2, x2 = (y + dy) % Y, (c + dc) % C, (x + dx) % X
        return y2, c2, x2, ((y2 * Z + z) * C + c2, x2)

    peers = Y * C * X
    mine = (y * C + c) * X + x
    source = x * (Y * C) + y * C + c

    def remote(src, dst, ss, rs, dev):
        return pltpu.make_async_remote_copy(
            src_ref=src, dst_ref=dst, send_sem=ss, recv_sem=rs, device_id=dev, device_id_type=MESH
        )

    def local(src, dst, sem):
        return pltpu.make_async_copy(src, dst, sem)

    fetch_s = [local(samples.at[:, pl.ds(f * wide, wide)], sv.at[f], ssem.at[f]) for f in range(nf)]
    for copy in fetch_s:
        copy.start()
    fetch_g = local(gate, gv, wsem.at[0])
    fetch_g.start()
    nt = w1.shape[0]
    fetch_1 = [
        local(up.at[0, :, pl.ds(j * w1.shape[2], w1.shape[2])], w1.at[j], wsem.at[1 + j]) for j in range(nt)
    ]
    fetch_2 = [
        local(down.at[0, :, pl.ds(j * w2.shape[2], w2.shape[2])], w2.at[j], wsem.at[1 + nt + j]) for j in range(nt)
    ]
    for copy in fetch_1 + fetch_2:
        copy.start()

    barrier = pltpu.get_barrier_semaphore()

    def greet(k, carry):
        pl.semaphore_signal(barrier, inc=1, device_id=in_plane(k)[3], device_id_type=MESH)
        return carry

    lax.fori_loop(1, peers, greet, 0)
    for d in range(1, Z):
        pl.semaphore_signal(barrier, inc=1, device_id=at_z(d), device_id_type=MESH)
    pl.semaphore_wait(barrier, peers - 1 + Z - 1)

    sign = (1, -1)

    def hop_copy(step, way, f):
        dev = at_z(sign[way])
        sems = hsend.at[way, step, f], hrecv.at[way, step, f]
        if step == 0:
            src, dst = sv.at[f], near.at[way, 0, f]
        elif step == 1:
            src, dst = near.at[way, 0, f], near.at[way, 1, f]
        elif step == 2:
            src, dst = hop.at[way, f], far.at[way, f]
        else:
            src, dst = far.at[way, f, pl.ds(0, half)], last.at[way, f]
        return remote(src, dst, *sems, dev)

    for f in range(nf):
        fetch_s[f].wait()
        if f == 0:
            hop_copy(0, 0, 0).start()
            hop_copy(0, 1, 0).start()

    experts = gate.shape[1]
    earlier = as_mask(iota((rows, rows), 0) < iota((rows, rows), 1))
    named = [as_mask(iota((experts, rows), 0) == ids[k : k + 1, :]) for k in range(2)]
    count = jnp.dot((named[0].astype(F32) + named[1].astype(F32)).astype(BF16), earlier, **EXACT)
    rowb[...] = jnp.zeros_like(rowb)
    for k in range(2):
        rank = jnp.sum(named[k].astype(F32) * count, axis=0, keepdims=True)
        posb[0, k : k + 1, :] = ids[k : k + 1, :] * CAP + rank.astype(I32)
        rowb[k : k + 1, :] = ids[k : k + 1, :].astype(F32)
        rowb[2 + k : 3 + k, :] = rank
    rowb[4:5, :] = mask[...].astype(F32)

    def pos_copy(d):
        return remote(posb.at[0], posb.at[d], msend.at[0], mrecv.at[0], at_z(d))

    for d in range(1, Z):
        pos_copy(d).start()
    for f in range(1, nf):
        hop_copy(0, 0, f).start()
        hop_copy(0, 1, f).start()

    same = as_mask(iota((rows, rows), 0) == iota((rows, rows), 1))
    turned = lax.dot_general(same, rowb[...].astype(BF16), (((1,), (1,)), ((), ())), **EXACT)
    cols[...] = turned.reshape(cols.shape)

    def target(shape, dim, n, a, plane):
        i = iota(shape, dim)
        if n == CAP:
            block, j = div(i, CAP * C * X), i
            return block * (Z * C * X * CAP - C * X * CAP) + plane * (C * X * CAP) + j
        d = div(i, n)
        s = i - d * n - a * CAP
        block = lax.shift_right_logical(d, 3)
        slot = block * (Z * C * X * CAP) + plane * (C * X * CAP) + (d - block * (C * X)) * CAP + s
        return jnp.where((s >= 0) & (s < CAP), slot, -1)

    def chooser(slots, d):
        p0, p1 = posb[d, 0:1, :], posb[d, 1:2, :]
        return as_mask((slots == p0) | (slots == p1))

    def send_in_plane(g):
        def one(k, carry):
            y2, c2, x2, dev = in_plane(k)
            remote(sb[g].at[(y2 * C + c2) * X + x2], xb[g].at[source], isend.at[g], irecv.at[g], dev).start()
            return carry

        lax.fori_loop(1, peers, one, 0)
        xb[g][source] = sb[g][mine]

    def put(g, f, value):
        n = width[g]
        sb[g][:, :, f * wide : (f + 1) * wide] = value.reshape(peers, n, wide).astype(BF16)

    pick[0, : peers * 16, :] = chooser(target((peers * 16, 1), 0, 16, 0, z), 0)
    for f in range(nf):
        put(0, f, jnp.dot(pick[0, : peers * 16, :], sv[f], **EXACT))
    send_in_plane(0)

    fetch_g.wait()
    logits = jnp.zeros((rows, experts), F32)
    for f in range(nf):
        logits = logits + jnp.dot(sv[f], gv[f * wide : (f + 1) * wide, :], **EXACT)
    lpart[...] = logits.reshape(lpart.shape)

    def along_x(d):
        return ne, (x + d) % X

    def logit_copy(d):
        return remote(lpart.at[(x + d) % X], lrecv.at[d - 1], msend.at[1], mrecv.at[1], along_x(d))

    for d in range(1, X):
        logit_copy(d).start()

    def relay(step, f):
        for way in range(2):
            hop_copy(step, way, f).wait_recv()
            if step < 3:
                hop_copy(step + 1, way, f).start()

    m_of = [Y * C * n for n in width]

    def expert(g):
        n, m = width[g], m_of[g]
        remote(sb[g].at[pl.ds(0, peers - 1)], xb[g].at[pl.ds(0, peers - 1)], isend.at[g], irecv.at[g], along_x(1)).wait_recv()

        def first(j, carry):
            total = jnp.zeros((m, w1.shape[2]), F32)
            for xs in range(X):
                part = xb[g][xs * Y * C : (xs + 1) * Y * C].reshape(m, nf * wide)
                total = total + jnp.dot(part, w1[j, xs * nf * wide : (xs + 1) * nf * wide, :], **EXACT)
            act[j, 0:m, :] = jnp.maximum(total, 0.0).astype(BF16)
            return carry

        lax.fori_loop(0, nt, first, 0)

        def second(j, carry):
            total = jnp.zeros((m, w2.shape[2]), F32)
            for i in range(nt):
                total = total + jnp.dot(act[i, 0:m, :], w2[j, i * w1.shape[2] : (i + 1) * w1.shape[2], :], **EXACT)
            ob[g][j] = total.reshape(Y * C, n, w2.shape[2]).astype(BF16)
            return carry

        lax.fori_loop(0, nt, second, 0)

        def one(k, carry):
            y2, c2, x2, dev = in_plane(k)
            remote(ob[g].at[x2, y2 * C + c2], rb[g].at[mine], rsend.at[g], rrecv.at[g], dev).start()
            return carry

        lax.fori_loop(1, peers, one, 0)
        rb[g][mine] = ob[g][x, y * C + c]

    def back_in_plane(g):
        block = rb[g].at[pl.ds(0, peers - 1)]
        remote(block, block, rsend.at[g], rrecv.at[g], along_x(1)).wait_recv()

    def back_copy(d):
        return remote(zs.at[d], zr.at[d], zsend.at[d], zrecv.at[d], at_z(-d))

    def send_back(g, sources):
        n = width[g]
        q, i = iota((2 * half, peers * n), 0), iota((2 * half, peers * n), 1)
        base = q + div(q, CAP) * (n - CAP)
        got = rb[g][...].reshape(peers * n, rb[g].shape[2])
        for a, d in enumerate(sources):
            zs[d] = jnp.dot(as_mask(i == base + a * CAP), got, **EXACT).astype(BF16)
            back_copy(d).start()

    def add_up(plane, n, values, fresh=False):
        slots = target((1, values.shape[0]), 1, n, 0, plane)
        for k in range(2):
            col = cols[...].reshape(rows, 8)
            p = (col[:, k : k + 1] * CAP + col[:, 2 + k : 3 + k]).astype(I32)
            term = jnp.dot(as_mask(p == slots), values, **EXACT)
            if fresh:
                acc[k] = term
            else:
                acc[k] += term

    relay(0, 0)
    relay(0, 1)
    for copy in fetch_1 + fetch_2:
        copy.wait()
    expert(0)
    relay(0, 2)
    relay(0, 3)
    remote(posb.at[pl.ds(0, Z - 1)], posb.at[pl.ds(0, Z - 1)], msend.at[0], mrecv.at[0], along_x(1)).wait_recv()

    def choose_pair(g, dist):
        n = width[g]
        for a, d in enumerate((dist, Z - dist)):
            pick[a] = chooser(target((peers * n, 1), 0, n, a, z), d)
        for f in range(nf):
            put(
                g, f,
                jnp.dot(pick[0], near[0, dist - 1, f], **EXACT) + jnp.dot(pick[1], near[1, dist - 1, f], **EXACT),
            )
        send_in_plane(g)

    choose_pair(1, 1)

    for way in range(2):
        d = 2 if way == 0 else Z - 2
        p3, p4 = (z + sign[way]) % Z, (z + 2 * sign[way]) % Z
        q4 = target((2 * half, 1), 0, CAP, 0, p4)
        pickr[way, 0:half, :] = chooser(q4[way * half : (way + 1) * half], d)
        pickr[way, half:, :] = chooser(target((2 * half, 1), 0, CAP, 0, p3), d)

    remote(lrecv, lrecv, msend.at[1], mrecv.at[1], along_x(1)).wait_recv()
    logit = lpart[x] + lrecv[0] + lrecv[1] + lrecv[2]
    row_top = jnp.max(logit, axis=1, keepdims=True)
    term = jnp.exp(logit - row_top)
    row_total = jnp.sum(term, axis=1, keepdims=True)
    col = cols[x]
    lane = iota((share, experts), 1)
    both = []
    for k in range(2):
        chosen = jnp.sum(jnp.where(lane == col[:, k : k + 1].astype(I32), term, 0.0), axis=1, keepdims=True)
        both.append(experts * chosen / row_total * col[:, 4:5])
    wide_lane = iota((share, fac.shape[2]), 1)
    fac[x] = jnp.where(wide_lane == 0, both[0], jnp.where(wide_lane == 1, both[1], 0.0))

    def factor_copy(d):
        return remote(fac.at[x], fac.at[x], msend.at[2], mrecv.at[2], along_x(d))

    for d in range(1, X):
        factor_copy(d).start()

    back_in_plane(0)
    add_up(z, 16, rb[0][...].reshape(peers * 16, rb[0].shape[2]), True)

    def relay_chosen(f):
        for way in range(2):
            hop_copy(1, way, f).wait_recv()
            hop[way, f] = jnp.dot(pickr[way], near[way, 1, f], **EXACT).astype(BF16)
            hop_copy(2, way, f).start()

    relay_chosen(0)
    relay_chosen(1)
    expert(1)
    relay_chosen(2)
    relay_chosen(3)
    back_in_plane(1)
    send_back(1, (1, Z - 1))
    choose_pair(2, 2)
    relay(2, 0)
    relay(2, 1)
    expert(2)
    relay(2, 2)
    relay(2, 3)

    def spread(n, a, count):
        i, q = iota((count // CAP * n, count), 0), iota((count // CAP * n, count), 1)
        return as_mask(i == q + div(q, CAP) * (n - CAP) + a * CAP)

    for a in range(2):
        pick[a, :, 0 : 2 * half] = spread(24, a, 2 * half)
    for f in range(nf):
        put(
            3, f,
            jnp.dot(pick[0, :, 0 : 2 * half], far[0, f, half:], **EXACT)
            + jnp.dot(pick[1, :, 0 : 2 * half], far[1, f, half:], **EXACT),
        )
    send_in_plane(3)
    back_in_plane(2)
    send_back(2, (2, Z - 2))

    relay(3, 0)
    relay(3, 1)
    relay(3, 2)
    relay(3, 3)
    grow = spread(16, 0, half)
    for f in range(nf):
        for way in range(2):
            half_peers = peers // 2
            sb[4][way * half_peers : (way + 1) * half_peers, :, f * wide : (f + 1) * wide] = (
                jnp.dot(grow, last[way, f], **EXACT).reshape(half_peers, 16, wide).astype(BF16)
            )
    send_in_plane(4)
    expert(3)
    back_in_plane(3)
    send_back(3, (3, Z - 3))
    expert(4)
    back_in_plane(4)
    send_back(4, (4,))

    for d in (1, 7, 2, 6, 3, 5, 4):
        back_copy(d).wait_recv()
        add_up((z + d) % Z, CAP, zr[d])

    block = fac.at[pl.ds(0, X - 1)]
    remote(block, block, msend.at[2], mrecv.at[2], along_x(1)).wait_recv()
    scale = fac[...].reshape(rows, fac.shape[2])
    out[...] = (scale[:, 0:1] * acc[0] + scale[:, 1:2] * acc[1]).astype(out.dtype)

    for step in range(4):
        for way in range(2):
            for f in range(nf):
                hop_copy(step, way, f).wait_send()
    remote(posb.at[pl.ds(0, Z - 1)], posb.at[pl.ds(0, Z - 1)], msend.at[0], mrecv.at[0], along_x(1)).wait_send()
    remote(lrecv, lrecv, msend.at[1], mrecv.at[1], along_x(1)).wait_send()
    remote(block, block, msend.at[2], mrecv.at[2], along_x(1)).wait_send()
    for g in range(5):
        sent = sb[g].at[pl.ds(0, peers - 1)]
        remote(sent, sent, isend.at[g], irecv.at[g], along_x(1)).wait_send()
        sent = rb[g].at[pl.ds(0, peers - 1)]
        remote(sent, sent, rsend.at[g], rrecv.at[g], along_x(1)).wait_send()
    for d in range(1, Z):
        back_copy(d).wait_send()


def per_device(samples, gate_weight, expert_ids, pad_mask, up_weight, down_weight):
    rows, share = samples.shape
    experts = gate_weight.shape[1]
    depth, hidden = up_weight.shape[1:]
    columns = down_weight.shape[2] // X
    peers = Y * C * X
    nf = 4
    wide = share // nf
    width = (16, 24, 24, 24, 16)
    slots = peers * CAP
    dma = pltpu.SemaphoreType.DMA
    any_space = pl.BlockSpec(memory_space=pl.ANY)
    vmem = pl.BlockSpec(memory_space=pltpu.VMEM)
    scratch = [
        pltpu.VMEM((nf, rows, wide), BF16),
        pltpu.VMEM(gate_weight.shape, BF16),
        pltpu.VMEM((4, depth, hidden // 4), BF16),
        pltpu.VMEM((4, hidden, columns), BF16),
        pltpu.VMEM((2, 2, nf, rows, wide), BF16),
        pltpu.VMEM((2, nf, slots * 3 // 2, wide), BF16),
        pltpu.VMEM((2, nf, slots * 3 // 2, wide), BF16),
        pltpu.VMEM((2, nf, slots // 2, wide), BF16),
    ]
    scratch += [pltpu.VMEM((peers, n, share), BF16) for n in width]
    scratch += [pltpu.VMEM((peers, n, share), BF16) for n in width]
    scratch += [pltpu.VMEM((X, Y * C, n, columns), BF16) for n in width]
    scratch += [pltpu.VMEM((peers, n, columns), BF16) for n in width]
    scratch += [
        pltpu.VMEM((Z, slots, columns), BF16),
        pltpu.VMEM((Z, slots, columns), BF16),
        pltpu.VMEM((Z, 2, rows), I32),
        pltpu.VMEM((8, rows), F32),
        pltpu.VMEM((2, peers * 24, rows), BF16),
        pltpu.VMEM((2, slots * 3 // 2, rows), BF16),
        pltpu.VMEM((X, rows // X, 8), F32),
        pltpu.VMEM((X, rows // X, experts), F32),
        pltpu.VMEM((X - 1, rows // X, experts), F32),
        pltpu.VMEM((X, rows // X, 128), F32),
        pltpu.VMEM((4, Y * C * 24, hidden // 4), BF16),
        pltpu.VMEM((2, rows, columns), F32),
    ]
    scratch += [
        dma((9,)), dma((nf,)), dma((2, 4, nf)), dma((2, 4, nf)), dma((5,)), dma((5,)),
        dma((5,)), dma((5,)), dma((Z,)), dma((Z,)), dma((3,)), dma((3,)),
    ]
    return pl.pallas_call(
        kernel,
        out_shape=jax.ShapeDtypeStruct((rows, columns), BF16),
        in_specs=[any_space, any_space, vmem, vmem, any_space, any_space],
        out_specs=vmem,
        scratch_shapes=scratch,
        compiler_params=pltpu.CompilerParams(
            collective_id=0, has_side_effects=True, vmem_limit_bytes=67043328
        ),
    )(samples, gate_weight, expert_ids.T, pad_mask.reshape(1, rows), up_weight, down_weight)


def solution(mesh):
    placed = (
        P("expert", "gate"),
        P("gate", None),
        P("expert", None),
        P("expert"),
        P(("expert", "gate"), None, None),
        P(("expert", "gate"), None, None),
    )
    return jax.shard_map(
        per_device, mesh=mesh, in_specs=placed, out_specs=P("expert", "gate"), check_vma=False
    )
```

time: 393 us -> 193 us (0.49); the launches traced: 386 us -> 193 us
  waiting for transfers between devices: 195 us -> 0 us
  Pallas kernels: 0 us -> 190 us
  local copies, waits for them, and re-layouts: 107 us -> 3.03 us
  blocking collectives: 30.9 us -> 0 us
  starting transfers between devices: 28.2 us -> 0 us
  matrix products: 17.5 us -> 0 us
  other arithmetic: 6.29 us -> 0 us
    all_to_all x3 -> x0, waiting for transfers between devices: 195 us -> none  [the longest x2 195 us: joined_exchange(): parts = lax.all_to_all(parts, axis, split_axis=0, concat_axis=0, tiled=True)]
    pallas_call x0 -> x1, Pallas kernels: none -> 190 us  [per_device(): pl.pallas_call(kernel, out_shape=jax.ShapeDtypeStruct((rows, columns), BF...]
    gather x5 -> x0, local copies, waits for them, and re-layouts: 35.6 us -> none  [the longest x1 17.6 us: per_device(): padded[owners].reshape(group_count, gate_count, capacity, feature_share)]
    all_gather x3 -> x0, blocking collectives: 30.9 us -> none  [joined(): everything = jax.tree.map(lambda part: lax.all_gather(part, axis), shard)]
    all_to_all x3 -> x0, starting transfers between devices: 28.2 us -> none  [the longest x2 24.6 us: joined_exchange(): parts = lax.all_to_all(parts, axis, split_axis=0, concat_axis=0, tiled=True)]
    reshape x3 -> x1, local copies, waits for them, and re-layouts: 22 us -> 1.27 us  [per_device(): pad_mask.reshape(1, rows)]
    another operation x5 -> x0, local copies, waits for them, and re-layouts: 20.4 us -> none  [the longest x1 10.6 us: joined_exchange(): parts = parts.reshape(-1, *inside)]
    dot_general x2 -> x0, matrix products: 17.5 us -> none  [the longest x1 14.6 us: per_device(): jnp.dot(active, down_weight[0], preferred_element_type=jnp.float32)]
  transfers between devices with their start and end apart: 3 -> 0, of which waited for: 2 -> 0; matrix products, arithmetic and copies ran while one was open for 18% -> 0% of each run, Pallas kernels for 0% -> 0%
where the time goes in v1:
time: 193 us
  Pallas kernels  190 us (98%)
  local copies, waits for them, and re-layouts  3.03 us (2%)
    pallas_call x1, Pallas kernels, per_device(): pl.pallas_call(kernel, out_shape=jax.ShapeDtypeStruct((rows, columns), BF...  190 us

profile of v1, /device:TPU:1, one launch (start us, length us, event | category | flops | bytes accessed | tf_op | source)
XLA Modules:
  0.0 192.7 jit_solution(3672144390387862351)
XLA Ops:
  0.0 1.3 reshape.3.mask
  1.3 189.7 %shard_map.64 = bf16[768,256]{1,0:T(8,128)(2,1)} custom-call(bf16[768,1024]{1,0:T(8,128)(2,1)} %samples.1, bf16[1024,256]{1,0:T(8,128)(2,1)} %gate.1, s32[2,768]{1,0:T(2,128)} %bitcast.1, s32[1,768]{1,0:T(1,128)} %reshape.3.mask, bf16[1,4096,1024]{2,1,0:T(8,128)(2,1)} %up.1, bf16[1,1024,1024]{2,1,0:T(8,128)(2,1)} %down.1), custom_call_target="tpu_custom_call" | custom-call | tf_op jit(solution)/shard_map/pallas_call | solution.py:432
  191.0 1.8 copy.8

commit v2 on v1

--- a/solution.py
+++ b/solution.py
@@ -1,5 +1,3 @@
-import functools
-
 import jax
 import jax.numpy as jnp
 from jax import lax
@@ -90,7 +88,8 @@
     lax.fori_loop(1, peers, greet, 0)
     for d in range(1, Z):
         pl.semaphore_signal(barrier, inc=1, device_id=at_z(d), device_id_type=MESH)
-    pl.semaphore_wait(barrier, peers - 1 + Z - 1)
+    with jax.named_scope("greet"):
+        pl.semaphore_wait(barrier, peers - 1 + Z - 1)
 
     sign = (1, -1)
 
@@ -153,23 +152,30 @@
         p0, p1 = posb[d, 0:1, :], posb[d, 1:2, :]
         return as_mask((slots == p0) | (slots == p1))
 
-    def send_in_plane(g):
+    def put(g, f, value):
+        sb[g][f] = value.reshape(peers, width[g], wide).astype(BF16)
+
+    def send_in_plane(g, f):
         def one(k, carry):
             y2, c2, x2, dev = in_plane(k)
-            remote(sb[g].at[(y2 * C + c2) * X + x2], xb[g].at[source], isend.at[g], irecv.at[g], dev).start()
+            to = (y2 * C + c2) * X + x2
+            remote(sb[g].at[f, to], xb[g].at[f, source], isend.at[g, f], irecv.at[g, f], dev).start()
             return carry
 
         lax.fori_loop(1, peers, one, 0)
-        xb[g][source] = sb[g][mine]
-
-    def put(g, f, value):
-        n = width[g]
-        sb[g][:, :, f * wide : (f + 1) * wide] = value.reshape(peers, n, wide).astype(BF16)
+        xb[g][f, source] = sb[g][f, mine]
+
+    def dispatched(g, f):
+        part = xb[g].at[f, pl.ds(0, peers - 1)]
+        return remote(part, part, isend.at[g, f], irecv.at[g, f], along_x(1))
+
+    def along_x(d):
+        return ne, (x + d) % X
 
     pick[0, : peers * 16, :] = chooser(target((peers * 16, 1), 0, 16, 0, z), 0)
     for f in range(nf):
         put(0, f, jnp.dot(pick[0, : peers * 16, :], sv[f], **EXACT))
-    send_in_plane(0)
+        send_in_plane(0, f)
 
     fetch_g.wait()
     logits = jnp.zeros((rows, experts), F32)
@@ -177,31 +183,24 @@
         logits = logits + jnp.dot(sv[f], gv[f * wide : (f + 1) * wide, :], **EXACT)
     lpart[...] = logits.reshape(lpart.shape)
 
-    def along_x(d):
-        return ne, (x + d) % X
-
     def logit_copy(d):
         return remote(lpart.at[(x + d) % X], lrecv.at[d - 1], msend.at[1], mrecv.at[1], along_x(d))
 
     for d in range(1, X):
         logit_copy(d).start()
 
-    def relay(step, f):
-        for way in range(2):
-            hop_copy(step, way, f).wait_recv()
-            if step < 3:
-                hop_copy(step + 1, way, f).start()
-
     m_of = [Y * C * n for n in width]
 
     def expert(g):
         n, m = width[g], m_of[g]
-        remote(sb[g].at[pl.ds(0, peers - 1)], xb[g].at[pl.ds(0, peers - 1)], isend.at[g], irecv.at[g], along_x(1)).wait_recv()
+        for f in range(nf):
+            dispatched(g, f).wait_recv()
 
         def first(j, carry):
             total = jnp.zeros((m, w1.shape[2]), F32)
             for xs in range(X):
-                part = xb[g][xs * Y * C : (xs + 1) * Y * C].reshape(m, nf * wide)
+                group = slice(xs * Y * C, (xs + 1) * Y * C)
+                part = jnp.concatenate([xb[g][f, group].reshape(m, wide) for f in range(nf)], axis=1)
                 total = total + jnp.dot(part, w1[j, xs * nf * wide : (xs + 1) * nf * wide, :], **EXACT)
             act[j, 0:m, :] = jnp.maximum(total, 0.0).astype(BF16)
             return carry
@@ -252,27 +251,65 @@
             else:
                 acc[k] += term
 
-    relay(0, 0)
-    relay(0, 1)
-    for copy in fetch_1 + fetch_2:
-        copy.wait()
-    expert(0)
-    relay(0, 2)
-    relay(0, 3)
     remote(posb.at[pl.ds(0, Z - 1)], posb.at[pl.ds(0, Z - 1)], msend.at[0], mrecv.at[0], along_x(1)).wait_recv()
 
     def choose_pair(g, dist):
         n = width[g]
         for a, d in enumerate((dist, Z - dist)):
             pick[a] = chooser(target((peers * n, 1), 0, n, a, z), d)
-        for f in range(nf):
-            put(
-                g, f,
-                jnp.dot(pick[0], near[0, dist - 1, f], **EXACT) + jnp.dot(pick[1], near[1, dist - 1, f], **EXACT),
+
+    def put_pair(g, dist, f):
+        put(
+            g, f,
+            jnp.dot(pick[0], near[0, dist - 1, f], **EXACT) + jnp.dot(pick[1], near[1, dist - 1, f], **EXACT),
+        )
+        send_in_plane(g, f)
+
+    def first_hop(f):
+        for way in range(2):
+            hop_copy(0, way, f).wait_recv()
+            hop_copy(1, way, f).start()
+        put_pair(1, 1, f)
+
+    def second_hop(f):
+        for way in range(2):
+            hop_copy(1, way, f).wait_recv()
+            hop[way, f] = jnp.dot(pickr[way], near[way, 1, f], **EXACT).astype(BF16)
+            hop_copy(2, way, f).start()
+        put_pair(2, 2, f)
+
+    def spread(n, a, count):
+        i, q = iota((count // CAP * n, count), 0), iota((count // CAP * n, count), 1)
+        return as_mask(i == q + div(q, CAP) * (n - CAP) + a * CAP)
+
+    def third_hop(f):
+        for way in range(2):
+            hop_copy(2, way, f).wait_recv()
+            hop_copy(3, way, f).start()
+        put(
+            3, f,
+            jnp.dot(pick[0, :, 0 : 2 * half], far[0, f, half:], **EXACT)
+            + jnp.dot(pick[1, :, 0 : 2 * half], far[1, f, half:], **EXACT),
+        )
+        send_in_plane(3, f)
+
+    def fourth_hop(f):
+        half_peers = peers // 2
+        grow = pick[0, 0 : half_peers * 16, 2 * half : 3 * half]
+        for way in range(2):
+            hop_copy(3, way, f).wait_recv()
+            sb[4][f, way * half_peers : (way + 1) * half_peers] = (
+                jnp.dot(grow, last[way, f], **EXACT).reshape(half_peers, 16, wide).astype(BF16)
             )
-        send_in_plane(g)
+        send_in_plane(4, f)
 
     choose_pair(1, 1)
+    first_hop(0)
+    first_hop(1)
+    for copy in fetch_1 + fetch_2:
+        copy.wait()
+    expert(0)
+    first_hop(2)
 
     for way in range(2):
         d = 2 if way == 0 else Z - 2
@@ -304,64 +341,41 @@
     back_in_plane(0)
     add_up(z, 16, rb[0][...].reshape(peers * 16, rb[0].shape[2]), True)
 
-    def relay_chosen(f):
-        for way in range(2):
-            hop_copy(1, way, f).wait_recv()
-            hop[way, f] = jnp.dot(pickr[way], near[way, 1, f], **EXACT).astype(BF16)
-            hop_copy(2, way, f).start()
-
-    relay_chosen(0)
-    relay_chosen(1)
+    def gather_back(d):
+        back_copy(d).wait_recv()
+        add_up((z + d) % Z, CAP, zr[d])
+
+    first_hop(3)
+    choose_pair(2, 2)
+    second_hop(0)
     expert(1)
-    relay_chosen(2)
-    relay_chosen(3)
+    second_hop(1)
     back_in_plane(1)
     send_back(1, (1, Z - 1))
-    choose_pair(2, 2)
-    relay(2, 0)
-    relay(2, 1)
-    expert(2)
-    relay(2, 2)
-    relay(2, 3)
-
-    def spread(n, a, count):
-        i, q = iota((count // CAP * n, count), 0), iota((count // CAP * n, count), 1)
-        return as_mask(i == q + div(q, CAP) * (n - CAP) + a * CAP)
-
+    second_hop(2)
+    second_hop(3)
     for a in range(2):
         pick[a, :, 0 : 2 * half] = spread(24, a, 2 * half)
-    for f in range(nf):
-        put(
-            3, f,
-            jnp.dot(pick[0, :, 0 : 2 * half], far[0, f, half:], **EXACT)
-            + jnp.dot(pick[1, :, 0 : 2 * half], far[1, f, half:], **EXACT),
-        )
-    send_in_plane(3)
+    pick[0, 0 : peers * 8, 2 * half : 3 * half] = spread(16, 0, half)
+    third_hop(0)
+    expert(2)
+    third_hop(1)
+    third_hop(2)
     back_in_plane(2)
     send_back(2, (2, Z - 2))
-
-    relay(3, 0)
-    relay(3, 1)
-    relay(3, 2)
-    relay(3, 3)
-    grow = spread(16, 0, half)
+    third_hop(3)
+    gather_back(1)
+    gather_back(Z - 1)
     for f in range(nf):
-        for way in range(2):
-            half_peers = peers // 2
-            sb[4][way * half_peers : (way + 1) * half_peers, :, f * wide : (f + 1) * wide] = (
-                jnp.dot(grow, last[way, f], **EXACT).reshape(half_peers, 16, wide).astype(BF16)
-            )
-    send_in_plane(4)
+        fourth_hop(f)
     expert(3)
+    expert(4)
     back_in_plane(3)
     send_back(3, (3, Z - 3))
-    expert(4)
     back_in_plane(4)
     send_back(4, (4,))
-
-    for d in (1, 7, 2, 6, 3, 5, 4):
-        back_copy(d).wait_recv()
-        add_up((z + d) % Z, CAP, zr[d])
+    for d in (2, 6, 3, 5, 4):
+        gather_back(d)
 
     block = fac.at[pl.ds(0, X - 1)]
     remote(block, block, msend.at[2], mrecv.at[2], along_x(1)).wait_recv()
@@ -376,8 +390,8 @@
     remote(lrecv, lrecv, msend.at[1], mrecv.at[1], along_x(1)).wait_send()
     remote(block, block, msend.at[2], mrecv.at[2], along_x(1)).wait_send()
     for g in range(5):
-        sent = sb[g].at[pl.ds(0, peers - 1)]
-        remote(sent, sent, isend.at[g], irecv.at[g], along_x(1)).wait_send()
+        for f in range(nf):
+            dispatched(g, f).wait_send()
         sent = rb[g].at[pl.ds(0, peers - 1)]
         remote(sent, sent, rsend.at[g], rrecv.at[g], along_x(1)).wait_send()
     for d in range(1, Z):
@@ -407,8 +421,8 @@
         pltpu.VMEM((2, nf, slots * 3 // 2, wide), BF16),
         pltpu.VMEM((2, nf, slots // 2, wide), BF16),
     ]
-    scratch += [pltpu.VMEM((peers, n, share), BF16) for n in width]
-    scratch += [pltpu.VMEM((peers, n, share), BF16) for n in width]
+    scratch += [pltpu.VMEM((nf, peers, n, wide), BF16) for n in width]
+    scratch += [pltpu.VMEM((nf, peers, n, wide), BF16) for n in width]
     scratch += [pltpu.VMEM((X, Y * C, n, columns), BF16) for n in width]
     scratch += [pltpu.VMEM((peers, n, columns), BF16) for n in width]
     scratch += [
@@ -426,7 +440,7 @@
         pltpu.VMEM((2, rows, columns), F32),
     ]
     scratch += [
-        dma((9,)), dma((nf,)), dma((2, 4, nf)), dma((2, 4, nf)), dma((5,)), dma((5,)),
+        dma((9,)), dma((nf,)), dma((2, 4, nf)), dma((2, 4, nf)), dma((5, nf)), dma((5, nf)),
         dma((5,)), dma((5,)), dma((Z,)), dma((Z,)), dma((3,)), dma((3,)),
     ]
     return pl.pallas_call(

time: 193 us -> 172 us (0.89)
  Pallas kernels: 190 us -> 168 us
    pallas_call x1, Pallas kernels: 190 us -> 168 us  [per_device(): pl.pallas_call(kernel, out_shape=jax.ShapeDtypeStruct((rows, columns), BF...]
where the time goes in v2:
time: 172 us; the launch traced here: 171 us
  Pallas kernels  168 us (98%)
  local copies, waits for them, and re-layouts  3.03 us (2%)
    pallas_call x1, Pallas kernels, per_device(): pl.pallas_call(kernel, out_shape=jax.ShapeDtypeStruct((rows, columns), BF...  168 us

profile of v2, /device:TPU:1, one launch (start us, length us, event | category | flops | bytes accessed | tf_op | source)
XLA Modules:
  0.0 171.4 jit_solution(4977001823819519896)
XLA Ops:
  0.0 1.3 reshape.3.mask
  1.3 168.3 %shard_map.64 = bf16[768,256]{1,0:T(8,128)(2,1)} custom-call(bf16[768,1024]{1,0:T(8,128)(2,1)} %samples.1, bf16[1024,256]{1,0:T(8,128)(2,1)} %gate.1, s32[2,768]{1,0:T(2,128)} %bitcast.1, s32[1,768]{1,0:T(1,128)} %reshape.3.mask, bf16[1,4096,1024]{2,1,0:T(8,128)(2,1)} %up.1, bf16[1,1024,1024]{2,1,0:T(8,128)(2,1)} %down.1), custom_call_target="tpu_custom_call" | custom-call | tf_op jit(solution)/shard_map/pallas_call | solution.py:446
  169.6 1.8 %copy.8 = bf16[768,256]{1,0:T(8,128)(2,1)} copy(bf16[768,256]{1,0:T(8,128)(2,1)} %shard_map.64) | data formatting | bytes 786432

commit v3 on v2

--- a/solution.py
+++ b/solution.py
@@ -29,7 +29,7 @@
     sv, gv, w1, w2, near, hop, far, last,
     sb0, sb1, sb2, sb3, sb4, xb0, xb1, xb2, xb3, xb4,
     ob0, ob1, ob2, ob3, ob4, rb0, rb1, rb2, rb3, rb4,
-    zs, zr, posb, rowb, pick, pickr, cols, lpart, lrecv, fac, act, acc,
+    zs, zr, posb, rowb, pick, pickr, cols, lpart, lrecv, fac, act, acc, hid,
     wsem, ssem, hsend, hrecv, isend, irecv, rsend, rrecv, zsend, zrecv, msend, mrecv,
 ):
     sb, xb = (sb0, sb1, sb2, sb3, sb4), (xb0, xb1, xb2, xb3, xb4)
@@ -44,15 +44,29 @@
     wide = sv.shape[2]
     share = rows // X
 
+    def up_z(d):
+        return lax.rem(z + d % Z, Z)
+
     def at_z(d):
-        return (y * Z + (z + d) % Z) * C + c, x
-
-    def in_plane(k):
-        dy, dc, dx = k // (C * X), (k // X) % C, k % X
-        y2, c2, x2 = (y + dy) % Y, (c + dc) % C, (x + dx) % X
-        return y2, c2, x2, ((y2 * Z + z) * C + c2, x2)
+        return (y * Z + up_z(d)) * C + c, x
 
     peers = Y * C * X
+
+    def to_plane(visit):
+        def one(i, k):
+            dc, dx = k % C, k // C
+            y2, c2, x2 = lax.rem(y + dx + i, Y), lax.rem(c + dc, C), lax.rem(x + dx, X)
+            visit(y2, c2, x2, ((y2 * Z + z) * C + c2, x2))
+
+        def some(i, carry):
+            for k in range(C * X):
+                one(i, k)
+            return carry
+
+        for k in range(1, C * X):
+            one(0, k)
+        lax.fori_loop(1, Y, some, 0)
+
     mine = (y * C + c) * X + x
     source = x * (Y * C) + y * C + c
 
@@ -60,6 +74,11 @@
         return pltpu.make_async_remote_copy(
             src_ref=src, dst_ref=dst, send_sem=ss, recv_sem=rs, device_id=dev, device_id_type=MESH
         )
+
+    barrier = pltpu.get_barrier_semaphore()
+    for d in (4, 3, 5, 2, 6, 1, 7):
+        pl.semaphore_signal(barrier, inc=1, device_id=at_z(d), device_id_type=MESH)
+    to_plane(lambda y2, c2, x2, dev: pl.semaphore_signal(barrier, inc=1, device_id=dev, device_id_type=MESH))
 
     def local(src, dst, sem):
         return pltpu.make_async_copy(src, dst, sem)
@@ -70,24 +89,18 @@
     fetch_g = local(gate, gv, wsem.at[0])
     fetch_g.start()
     nt = w1.shape[0]
+    hw, ow = w1.shape[4], w2.shape[2]
     fetch_1 = [
-        local(up.at[0, :, pl.ds(j * w1.shape[2], w1.shape[2])], w1.at[j], wsem.at[1 + j]) for j in range(nt)
+        local(up.at[xs, :, :, pl.ds(j * hw, hw)], w1.at[j, :, xs], wsem.at[1 + j * X + xs])
+        for j in range(nt)
+        for xs in range(X)
     ]
     fetch_2 = [
-        local(down.at[0, :, pl.ds(j * w2.shape[2], w2.shape[2])], w2.at[j], wsem.at[1 + nt + j]) for j in range(nt)
+        local(down.at[0, :, pl.ds(j * ow, ow)], w2.at[j], wsem.at[1 + nt * X + j]) for j in range(nt)
     ]
     for copy in fetch_1 + fetch_2:
         copy.start()
 
-    barrier = pltpu.get_barrier_semaphore()
-
-    def greet(k, carry):
-        pl.semaphore_signal(barrier, inc=1, device_id=in_plane(k)[3], device_id_type=MESH)
-        return carry
-
-    lax.fori_loop(1, peers, greet, 0)
-    for d in range(1, Z):
-        pl.semaphore_signal(barrier, inc=1, device_id=at_z(d), device_id_type=MESH)
     with jax.named_scope("greet"):
         pl.semaphore_wait(barrier, peers - 1 + Z - 1)
 
@@ -122,7 +135,7 @@
         posb[0, k : k + 1, :] = ids[k : k + 1, :] * CAP + rank.astype(I32)
         rowb[k : k + 1, :] = ids[k : k + 1, :].astype(F32)
         rowb[2 + k : 3 + k, :] = rank
-    rowb[4:5, :] = mask[...].astype(F32)
+    rowb[4:5, :] = mask[...].reshape(1, rows).astype(F32)
 
     def pos_copy(d):
         return remote(posb.at[0], posb.at[d], msend.at[0], mrecv.at[0], at_z(d))
@@ -156,13 +169,11 @@
         sb[g][f] = value.reshape(peers, width[g], wide).astype(BF16)
 
     def send_in_plane(g, f):
-        def one(k, carry):
-            y2, c2, x2, dev = in_plane(k)
+        def one(y2, c2, x2, dev):
             to = (y2 * C + c2) * X + x2
             remote(sb[g].at[f, to], xb[g].at[f, source], isend.at[g, f], irecv.at[g, f], dev).start()
-            return carry
-
-        lax.fori_loop(1, peers, one, 0)
+
+        to_plane(one)
         xb[g][f, source] = sb[g][f, mine]
 
     def dispatched(g, f):
@@ -170,7 +181,7 @@
         return remote(part, part, isend.at[g, f], irecv.at[g, f], along_x(1))
 
     def along_x(d):
-        return ne, (x + d) % X
+        return ne, lax.rem(x + d, X)
 
     pick[0, : peers * 16, :] = chooser(target((peers * 16, 1), 0, 16, 0, z), 0)
     for f in range(nf):
@@ -184,45 +195,75 @@
     lpart[...] = logits.reshape(lpart.shape)
 
     def logit_copy(d):
-        return remote(lpart.at[(x + d) % X], lrecv.at[d - 1], msend.at[1], mrecv.at[1], along_x(d))
+        return remote(lpart.at[lax.rem(x + d, X)], lrecv.at[d - 1], msend.at[1], mrecv.at[1], along_x(d))
 
     for d in range(1, X):
         logit_copy(d).start()
 
     m_of = [Y * C * n for n in width]
 
+    def features(g, f):
+        part = [xb[g][f, xs * Y * C : (xs + 1) * Y * C].reshape(m_of[g], wide) for xs in range(X)]
+        return jnp.concatenate(part, axis=1)
+
+    def layer_1(g, f, j):
+        return jnp.dot(features(g, f), w1[j, f].reshape(X * wide, hw), **EXACT)
+
+    def partly(g, f):
+        m = m_of[g]
+        dispatched(g, f).wait_recv()
+
+        def one(j, carry):
+            if f == 0:
+                hid[g - 3, j, 0:m, :] = layer_1(g, f, j)
+            else:
+                hid[g - 3, j, 0:m, :] += layer_1(g, f, j)
+            return carry
+
+        lax.fori_loop(0, nt, one, 0)
+
+    def outward(g):
+        n, m = width[g], m_of[g]
+
+        def second(j, carry):
+            whole = jnp.concatenate([act[i, 0:m, :] for i in range(nt)], axis=1)
+            total = jnp.dot(whole, w2[j], **EXACT)
+            ob[g][j] = total.reshape(Y * C, n, ow).astype(BF16)
+            return carry
+
+        lax.fori_loop(0, nt, second, 0)
+
+        def one(y2, c2, x2, dev):
+            remote(ob[g].at[x2, y2 * C + c2], rb[g].at[mine], rsend.at[g], rrecv.at[g], dev).start()
+
+        to_plane(one)
+        rb[g][mine] = ob[g][x, y * C + c]
+
     def expert(g):
-        n, m = width[g], m_of[g]
+        m = m_of[g]
         for f in range(nf):
             dispatched(g, f).wait_recv()
 
         def first(j, carry):
-            total = jnp.zeros((m, w1.shape[2]), F32)
-            for xs in range(X):
-                group = slice(xs * Y * C, (xs + 1) * Y * C)
-                part = jnp.concatenate([xb[g][f, group].reshape(m, wide) for f in range(nf)], axis=1)
-                total = total + jnp.dot(part, w1[j, xs * nf * wide : (xs + 1) * nf * wide, :], **EXACT)
+            total = layer_1(g, 0, j)
+            for f in range(1, nf):
+                total = total + layer_1(g, f, j)
             act[j, 0:m, :] = jnp.maximum(total, 0.0).astype(BF16)
             return carry
 
         lax.fori_loop(0, nt, first, 0)
-
-        def second(j, carry):
-            total = jnp.zeros((m, w2.shape[2]), F32)
-            for i in range(nt):
-                total = total + jnp.dot(act[i, 0:m, :], w2[j, i * w1.shape[2] : (i + 1) * w1.shape[2], :], **EXACT)
-            ob[g][j] = total.reshape(Y * C, n, w2.shape[2]).astype(BF16)
+        outward(g)
+
+    def finish(g):
+        m = m_of[g]
+        partly(g, nf - 1)
+
+        def first(j, carry):
+            act[j, 0:m, :] = jnp.maximum(hid[g - 3, j, 0:m, :], 0.0).astype(BF16)
             return carry
 
-        lax.fori_loop(0, nt, second, 0)
-
-        def one(k, carry):
-            y2, c2, x2, dev = in_plane(k)
-            remote(ob[g].at[x2, y2 * C + c2], rb[g].at[mine], rsend.at[g], rrecv.at[g], dev).start()
-            return carry
-
-        lax.fori_loop(1, peers, one, 0)
-        rb[g][mine] = ob[g][x, y * C + c]
+        lax.fori_loop(0, nt, first, 0)
+        outward(g)
 
     def back_in_plane(g):
         block = rb[g].at[pl.ds(0, peers - 1)]
@@ -313,7 +354,7 @@
 
     for way in range(2):
         d = 2 if way == 0 else Z - 2
-        p3, p4 = (z + sign[way]) % Z, (z + 2 * sign[way]) % Z
+        p3, p4 = up_z(sign[way]), up_z(2 * sign[way])
         q4 = target((2 * half, 1), 0, CAP, 0, p4)
         pickr[way, 0:half, :] = chooser(q4[way * half : (way + 1) * half], d)
         pickr[way, half:, :] = chooser(target((2 * half, 1), 0, CAP, 0, p3), d)
@@ -343,7 +384,7 @@
 
     def gather_back(d):
         back_copy(d).wait_recv()
-        add_up((z + d) % Z, CAP, zr[d])
+        add_up(up_z(d), CAP, zr[d])
 
     first_hop(3)
     choose_pair(2, 2)
@@ -360,21 +401,28 @@
     third_hop(0)
     expert(2)
     third_hop(1)
+    gather_back(1)
+    partly(3, 0)
     third_hop(2)
+    partly(3, 1)
     back_in_plane(2)
+    third_hop(3)
     send_back(2, (2, Z - 2))
-    third_hop(3)
-    gather_back(1)
-    gather_back(Z - 1)
-    for f in range(nf):
-        fourth_hop(f)
-    expert(3)
-    expert(4)
+    partly(3, 2)
+    fourth_hop(0)
+    fourth_hop(1)
+    finish(3)
+    fourth_hop(2)
+    fourth_hop(3)
+    partly(4, 0)
+    partly(4, 1)
     back_in_plane(3)
     send_back(3, (3, Z - 3))
+    partly(4, 2)
+    finish(4)
     back_in_plane(4)
     send_back(4, (4,))
-    for d in (2, 6, 3, 5, 4):
+    for d in (7, 2, 6, 3, 5, 4):
         gather_back(d)
 
     block = fac.at[pl.ds(0, X - 1)]
@@ -414,7 +462,7 @@
     scratch = [
         pltpu.VMEM((nf, rows, wide), BF16),
         pltpu.VMEM(gate_weight.shape, BF16),
-        pltpu.VMEM((4, depth, hidden // 4), BF16),
+        pltpu.VMEM((4, nf, X, wide, hidden // 4), BF16),
         pltpu.VMEM((4, hidden, columns), BF16),
         pltpu.VMEM((2, 2, nf, rows, wide), BF16),
         pltpu.VMEM((2, nf, slots * 3 // 2, wide), BF16),
@@ -438,9 +486,10 @@
         pltpu.VMEM((X, rows // X, 128), F32),
         pltpu.VMEM((4, Y * C * 24, hidden // 4), BF16),
         pltpu.VMEM((2, rows, columns), F32),
+        pltpu.VMEM((2, 4, Y * C * 24, hidden // 4), F32),
     ]
     scratch += [
-        dma((9,)), dma((nf,)), dma((2, 4, nf)), dma((2, 4, nf)), dma((5, nf)), dma((5, nf)),
+        dma((5 + 4 * X,)), dma((nf,)), dma((2, 4, nf)), dma((2, 4, nf)), dma((5, nf)), dma((5, nf)),
         dma((5,)), dma((5,)), dma((Z,)), dma((Z,)), dma((3,)), dma((3,)),
     ]
     return pl.pallas_call(
@@ -452,7 +501,8 @@
         compiler_params=pltpu.CompilerParams(
             collective_id=0, has_side_effects=True, vmem_limit_bytes=67043328
         ),
-    )(samples, gate_weight, expert_ids.T, pad_mask.reshape(1, rows), up_weight, down_weight)
+    )(samples, gate_weight, expert_ids.T, pad_mask,
+      up_weight.reshape(X, nf, wide, hidden), down_weight)
 
 
 def solution(mesh):

time: 172 us -> 163 us (0.948)
  Pallas kernels: 168 us -> 161 us
    pallas_call x1, Pallas kernels: 168 us -> 161 us  [per_device(): pl.pallas_call(kernel, out_shape=jax.ShapeDtypeStruct((rows, columns), BF...]
where the time goes in v3:
time: 163 us
  Pallas kernels  161 us (99%)
  local copies, waits for them, and re-layouts  1.77 us (1%)
    pallas_call x1, Pallas kernels, per_device(): pl.pallas_call(kernel, out_shape=jax.ShapeDtypeStruct((rows, columns), BF...  161 us

profile of v3, /device:TPU:1, one launch (start us, length us, event | category | flops | bytes accessed | tf_op | source)
XLA Modules:
  0.0 162.9 jit_solution(11652686824697895428)
XLA Ops:
  0.0 161.1 %shard_map.64 = bf16[768,256]{1,0:T(8,128)(2,1)} custom-call(bf16[768,1024]{1,0:T(8,128)(2,1)} %samples.1, bf16[1024,256]{1,0:T(8,128)(2,1)} %gate.1, s32[2,768]{1,0:T(2,128)} %bitcast.3, s32[768]{0:T(1024)} %mask.1, bf16[4,4,256,1024]{3,2,1,0:T(8,128)(2,1)} %bitcast.2, bf16[1,1024,1024]{2,1,0:T(8,128)(2,1)} %down.1), custom_call_target="tpu_custom_call" | custom-call | tf_op jit(solution)/shard_map/pallas_call | solution.py:495
  161.1 1.8 %copy.8 = bf16[768,256]{1,0:T(8,128)(2,1)} copy(bf16[768,256]{1,0:T(8,128)(2,1)} %shard_map.64) | data formatting | bytes 786432

commit v4 on v3

--- a/solution.py
+++ b/solution.py
@@ -29,8 +29,8 @@
     sv, gv, w1, w2, near, hop, far, last,
     sb0, sb1, sb2, sb3, sb4, xb0, xb1, xb2, xb3, xb4,
     ob0, ob1, ob2, ob3, ob4, rb0, rb1, rb2, rb3, rb4,
-    zs, zr, posb, rowb, pick, pickr, cols, lpart, lrecv, fac, act, acc, hid,
-    wsem, ssem, hsend, hrecv, isend, irecv, rsend, rrecv, zsend, zrecv, msend, mrecv,
+    zs, zr, posb, rowb, pick, pickr, cols, lpart, lrecv, fac, act, acc, hid, apart,
+    wsem, ssem, known, hsend, hrecv, isend, irecv, rsend, rrecv, zsend, zrecv, msend, mrecv,
 ):
     sb, xb = (sb0, sb1, sb2, sb3, sb4), (xb0, xb1, xb2, xb3, xb4)
     ob, rb = (ob0, ob1, ob2, ob3, ob4), (rb0, rb1, rb2, rb3, rb4)
@@ -76,9 +76,20 @@
         )
 
     barrier = pltpu.get_barrier_semaphore()
-    for d in (4, 3, 5, 2, 6, 1, 7):
-        pl.semaphore_signal(barrier, inc=1, device_id=at_z(d), device_id_type=MESH)
-    to_plane(lambda y2, c2, x2, dev: pl.semaphore_signal(barrier, inc=1, device_id=dev, device_id_type=MESH))
+    z_near = (at_z(1), at_z(-1))
+    y_near = tuple(((lax.rem(y + d, Y) * Z + z) * C + c, x) for d in (1, Y - 1))
+    x_near = tuple((ne, lax.rem(x + d, X)) for d in (1, X - 1))
+    partner = (((y * Z + z) * C + lax.rem(c + 1, C), x),)
+    neighbours = z_near + y_near + x_near + partner
+    for dev in neighbours:
+        pl.semaphore_signal(barrier, inc=1, device_id=dev, device_id_type=MESH)
+
+    def tell(i, devices):
+        for dev in devices:
+            pl.semaphore_signal(known.at[i], inc=1, device_id=dev, device_id_type=MESH)
+
+    def heard(i, devices):
+        pl.semaphore_wait(known.at[i], len(devices))
 
     def local(src, dst, sem):
         return pltpu.make_async_copy(src, dst, sem)
@@ -91,24 +102,24 @@
     nt = w1.shape[0]
     hw, ow = w1.shape[4], w2.shape[2]
     fetch_1 = [
-        local(up.at[xs, :, :, pl.ds(j * hw, hw)], w1.at[j, :, xs], wsem.at[1 + j * X + xs])
+        local(up.at[xs, :, :, pl.ds(j * hw, hw)], w1.at[j, :, xs], wsem.at[1])
         for j in range(nt)
         for xs in range(X)
     ]
     fetch_2 = [
-        local(down.at[0, :, pl.ds(j * ow, ow)], w2.at[j], wsem.at[1 + nt * X + j]) for j in range(nt)
+        local(down.at[0, :, pl.ds(j * ow, ow)], w2.at[j], wsem.at[2]) for j in range(nt)
     ]
     for copy in fetch_1 + fetch_2:
         copy.start()
 
     with jax.named_scope("greet"):
-        pl.semaphore_wait(barrier, peers - 1 + Z - 1)
+        pl.semaphore_wait(barrier, len(neighbours))
 
     sign = (1, -1)
 
     def hop_copy(step, way, f):
         dev = at_z(sign[way])
-        sems = hsend.at[way, step, f], hrecv.at[way, step, f]
+        sems = hsend.at[step], hrecv.at[way, step, f]
         if step == 0:
             src, dst = sv.at[f], near.at[way, 0, f]
         elif step == 1:
@@ -124,6 +135,8 @@
         if f == 0:
             hop_copy(0, 0, 0).start()
             hop_copy(0, 1, 0).start()
+            tell(0, x_near)
+            tell(1, z_near)
 
     experts = gate.shape[1]
     earlier = as_mask(iota((rows, rows), 0) < iota((rows, rows), 1))
@@ -140,7 +153,12 @@
     def pos_copy(d):
         return remote(posb.at[0], posb.at[d], msend.at[0], mrecv.at[0], at_z(d))
 
-    for d in range(1, Z):
+    heard(1, z_near)
+    tell(2, z_near)
+    heard(0, x_near)
+    tell(3, y_near)
+    near_z = (1, Z - 1, 2, Z - 2)
+    for d in near_z:
         pos_copy(d).start()
     for f in range(1, nf):
         hop_copy(0, 0, f).start()
@@ -149,6 +167,10 @@
     same = as_mask(iota((rows, rows), 0) == iota((rows, rows), 1))
     turned = lax.dot_general(same, rowb[...].astype(BF16), (((1,), (1,)), ((), ())), **EXACT)
     cols[...] = turned.reshape(cols.shape)
+    heard(3, y_near)
+    tell(4, y_near)
+    heard(2, z_near)
+    tell(5, z_near)
 
     def target(shape, dim, n, a, plane):
         i = iota(shape, dim)
@@ -171,22 +193,17 @@
     def send_in_plane(g, f):
         def one(y2, c2, x2, dev):
             to = (y2 * C + c2) * X + x2
-            remote(sb[g].at[f, to], xb[g].at[f, source], isend.at[g, f], irecv.at[g, f], dev).start()
+            remote(sb[g].at[f, to], xb[g].at[f, source], isend.at[g], irecv.at[g, f], dev).start()
 
         to_plane(one)
         xb[g][f, source] = sb[g][f, mine]
 
     def dispatched(g, f):
         part = xb[g].at[f, pl.ds(0, peers - 1)]
-        return remote(part, part, isend.at[g, f], irecv.at[g, f], along_x(1))
+        return remote(part, part, isend.at[g], irecv.at[g, f], along_x(1))
 
     def along_x(d):
         return ne, lax.rem(x + d, X)
-
-    pick[0, : peers * 16, :] = chooser(target((peers * 16, 1), 0, 16, 0, z), 0)
-    for f in range(nf):
-        put(0, f, jnp.dot(pick[0, : peers * 16, :], sv[f], **EXACT))
-        send_in_plane(0, f)
 
     fetch_g.wait()
     logits = jnp.zeros((rows, experts), F32)
@@ -200,6 +217,16 @@
     for d in range(1, X):
         logit_copy(d).start()
 
+    heard(4, y_near)
+    tell(6, partner)
+    heard(5, z_near)
+    pick[0, : peers * 16, :] = chooser(target((peers * 16, 1), 0, 16, 0, z), 0)
+    for f in range(nf):
+        put(0, f, jnp.dot(pick[0, : peers * 16, :], sv[f], **EXACT))
+        if f == 0:
+            heard(6, partner)
+        send_in_plane(0, f)
+
     m_of = [Y * C * n for n in width]
 
     def features(g, f):
@@ -207,11 +234,24 @@
         return jnp.concatenate(part, axis=1)
 
     def layer_1(g, f, j):
-        return jnp.dot(features(g, f), w1[j, f].reshape(X * wide, hw), **EXACT)
+        part = features(g, f) if g < 4 else apart[...]
+        return jnp.dot(part, w1[j, f].reshape(X * wide, hw), **EXACT)
 
     def partly(g, f):
         m = m_of[g]
-        dispatched(g, f).wait_recv()
+        if g < 4:
+            dispatched(g, f).wait_recv()
+        else:
+            h, a = f // 2, f % 2
+            if a == 0:
+                dispatched(g, h).wait_recv()
+            i, r = iota((m, Y * C * 24), 1), iota((m, Y * C * 24), 0)
+            p = lax.shift_right_logical(r, 4)
+            keep = (i == p * 24 + (r - p * 16) + a * CAP) & (r - p * 16 < CAP)
+            both = [xb[g][h, xs * Y * C : (xs + 1) * Y * C].reshape(Y * C * 24, wide) for xs in range(X)]
+            for xs in range(X):
+                part = jnp.dot(as_mask(keep), both[xs], **EXACT)
+                apart[:, xs * wide : (xs + 1) * wide] = part.astype(BF16)
 
         def one(j, carry):
             if f == 0:
@@ -224,19 +264,17 @@
 
     def outward(g):
         n, m = width[g], m_of[g]
-
-        def second(j, carry):
+        for dx in (2, 1, 3, 0):
+            x2 = lax.rem(x + dx, X)
             whole = jnp.concatenate([act[i, 0:m, :] for i in range(nt)], axis=1)
-            total = jnp.dot(whole, w2[j], **EXACT)
-            ob[g][j] = total.reshape(Y * C, n, ow).astype(BF16)
-            return carry
-
-        lax.fori_loop(0, nt, second, 0)
-
-        def one(y2, c2, x2, dev):
-            remote(ob[g].at[x2, y2 * C + c2], rb[g].at[mine], rsend.at[g], rrecv.at[g], dev).start()
-
-        to_plane(one)
+            total = jnp.dot(whole, w2[x2], **EXACT)
+            ob[g][x2] = total.reshape(Y * C, n, ow).astype(BF16)
+            for dy in (2, 1, 3, 0):
+                for dc in range(C):
+                    y2, c2 = lax.rem(y + dy, Y), lax.rem(c + dc, C)
+                    if dx + dy + dc:
+                        dev = (y2 * Z + z) * C + c2, x2
+                        remote(ob[g].at[x2, y2 * C + c2], rb[g].at[mine], rsend.at[g], rrecv.at[g], dev).start()
         rb[g][mine] = ob[g][x, y * C + c]
 
     def expert(g):
@@ -270,7 +308,7 @@
         remote(block, block, rsend.at[g], rrecv.at[g], along_x(1)).wait_recv()
 
     def back_copy(d):
-        return remote(zs.at[d], zr.at[d], zsend.at[d], zrecv.at[d], at_z(-d))
+        return remote(zs.at[d], zr.at[d], zsend.at[0], zrecv.at[d], at_z(-d))
 
     def send_back(g, sources):
         n = width[g]
@@ -292,7 +330,8 @@
             else:
                 acc[k] += term
 
-    remote(posb.at[pl.ds(0, Z - 1)], posb.at[pl.ds(0, Z - 1)], msend.at[0], mrecv.at[0], along_x(1)).wait_recv()
+    shared = posb.at[pl.ds(0, len(near_z))]
+    shared = remote(shared, shared, msend.at[0], mrecv.at[0], along_x(1))
 
     def choose_pair(g, dist):
         n = width[g]
@@ -310,6 +349,9 @@
         for way in range(2):
             hop_copy(0, way, f).wait_recv()
             hop_copy(1, way, f).start()
+        if f == 0:
+            shared.wait_recv()
+            choose_pair(1, 1)
         put_pair(1, 1, f)
 
     def second_hop(f):
@@ -334,21 +376,22 @@
         )
         send_in_plane(3, f)
 
-    def fourth_hop(f):
+    def fourth_hop(h):
         half_peers = peers // 2
-        grow = pick[0, 0 : half_peers * 16, 2 * half : 3 * half]
         for way in range(2):
-            hop_copy(3, way, f).wait_recv()
-            sb[4][f, way * half_peers : (way + 1) * half_peers] = (
-                jnp.dot(grow, last[way, f], **EXACT).reshape(half_peers, 16, wide).astype(BF16)
+            total = jnp.zeros((half_peers * 24, wide), F32)
+            for a in range(2):
+                hop_copy(3, way, 2 * h + a).wait_recv()
+                total = total + jnp.dot(pick[a, 0 : half_peers * 24, 0:half], last[way, 2 * h + a], **EXACT)
+            sb[4][h, way * half_peers : (way + 1) * half_peers] = (
+                total.reshape(half_peers, 24, wide).astype(BF16)
             )
-        send_in_plane(4, f)
-
-    choose_pair(1, 1)
+        send_in_plane(4, h)
+
     first_hop(0)
     first_hop(1)
-    for copy in fetch_1 + fetch_2:
-        copy.wait()
+    local(w1, w1, wsem.at[1]).wait()
+    local(w2, w2, wsem.at[2]).wait()
     expert(0)
     first_hop(2)
 
@@ -397,7 +440,11 @@
     second_hop(3)
     for a in range(2):
         pick[a, :, 0 : 2 * half] = spread(24, a, 2 * half)
-    pick[0, 0 : peers * 8, 2 * half : 3 * half] = spread(16, 0, half)
+    last_slots = target((1, 2 * half), 1, CAP, 0, up_z(4))
+    for k in range(2):
+        col = cols[...].reshape(rows, 8)
+        p = (col[:, k : k + 1] * CAP + col[:, 2 + k : 3 + k]).astype(I32)
+        pick[k, :, 2 * half : 4 * half] = as_mask(p == last_slots)
     third_hop(0)
     expert(2)
     third_hop(1)
@@ -410,10 +457,8 @@
     send_back(2, (2, Z - 2))
     partly(3, 2)
     fourth_hop(0)
+    finish(3)
     fourth_hop(1)
-    finish(3)
-    fourth_hop(2)
-    fourth_hop(3)
     partly(4, 0)
     partly(4, 1)
     back_in_plane(3)
@@ -422,28 +467,28 @@
     finish(4)
     back_in_plane(4)
     send_back(4, (4,))
-    for d in (7, 2, 6, 3, 5, 4):
+    for d in (7, 2, 6, 3, 5):
         gather_back(d)
 
     block = fac.at[pl.ds(0, X - 1)]
     remote(block, block, msend.at[2], mrecv.at[2], along_x(1)).wait_recv()
     scale = fac[...].reshape(rows, fac.shape[2])
-    out[...] = (scale[:, 0:1] * acc[0] + scale[:, 1:2] * acc[1]).astype(out.dtype)
-
-    for step in range(4):
-        for way in range(2):
-            for f in range(nf):
-                hop_copy(step, way, f).wait_send()
-    remote(posb.at[pl.ds(0, Z - 1)], posb.at[pl.ds(0, Z - 1)], msend.at[0], mrecv.at[0], along_x(1)).wait_send()
+    for step, whole in enumerate((near.at[:, 0], near.at[:, 1], hop, last)):
+        remote(whole, whole, hsend.at[step], hrecv.at[0, step, 0], at_z(1)).wait_send()
+    shared.wait_send()
     remote(lrecv, lrecv, msend.at[1], mrecv.at[1], along_x(1)).wait_send()
     remote(block, block, msend.at[2], mrecv.at[2], along_x(1)).wait_send()
     for g in range(5):
-        for f in range(nf):
-            dispatched(g, f).wait_send()
+        sent = xb[g].at[:, pl.ds(0, peers - 1)]
+        remote(sent, sent, isend.at[g], irecv.at[g, 0], along_x(1)).wait_send()
         sent = rb[g].at[pl.ds(0, peers - 1)]
         remote(sent, sent, rsend.at[g], rrecv.at[g], along_x(1)).wait_send()
-    for d in range(1, Z):
-        back_copy(d).wait_send()
+    sent = zs.at[pl.ds(1, Z - 1)]
+    remote(sent, sent, zsend.at[0], zrecv.at[1], at_z(1)).wait_send()
+
+    back_copy(4).wait_recv()
+    final = [acc[k] + jnp.dot(pick[k, :, 2 * half : 4 * half], zr[4], **EXACT) for k in range(2)]
+    out[...] = (scale[:, 0:1] * final[0] + scale[:, 1:2] * final[1]).astype(out.dtype)
 
 
 def per_device(samples, gate_weight, expert_ids, pad_mask, up_weight, down_weight):
@@ -469,8 +514,8 @@
         pltpu.VMEM((2, nf, slots * 3 // 2, wide), BF16),
         pltpu.VMEM((2, nf, slots // 2, wide), BF16),
     ]
-    scratch += [pltpu.VMEM((nf, peers, n, wide), BF16) for n in width]
-    scratch += [pltpu.VMEM((nf, peers, n, wide), BF16) for n in width]
+    messages = [(nf, peers, n, wide) for n in width[:4]] + [(nf // 2, peers, 24, wide)]
+    scratch += [pltpu.VMEM(shape, BF16) for shape in messages * 2]
     scratch += [pltpu.VMEM((X, Y * C, n, columns), BF16) for n in width]
     scratch += [pltpu.VMEM((peers, n, columns), BF16) for n in width]
     scratch += [
@@ -487,10 +532,11 @@
         pltpu.VMEM((4, Y * C * 24, hidden // 4), BF16),
         pltpu.VMEM((2, rows, columns), F32),
         pltpu.VMEM((2, 4, Y * C * 24, hidden // 4), F32),
+        pltpu.VMEM((Y * C * 16, depth // 4), BF16),
     ]
     scratch += [
-        dma((5 + 4 * X,)), dma((nf,)), dma((2, 4, nf)), dma((2, 4, nf)), dma((5, nf)), dma((5, nf)),
-        dma((5,)), dma((5,)), dma((Z,)), dma((Z,)), dma((3,)), dma((3,)),
+        dma((3,)), dma((nf,)), pltpu.SemaphoreType.REGULAR((7,)), dma((4,)), dma((2, 4, nf)), dma((5,)), dma((5, nf)),
+        dma((5,)), dma((5,)), dma((1,)), dma((Z,)), dma((3,)), dma((3,)),
     ]
     return pl.pallas_call(
         kernel,

time: 163 us -> 159 us (0.975)
  Pallas kernels: 161 us -> 156 us
    pallas_call x1, Pallas kernels: 161 us -> 156 us  [per_device(): pl.pallas_call(kernel, out_shape=jax.ShapeDtypeStruct((rows, columns), BF...]
where the time goes in v4:
time: 159 us; the launch traced here: 158 us
  Pallas kernels  156 us (98%)
  local copies, waits for them, and re-layouts  1.77 us (1%)
    pallas_call x1, Pallas kernels, per_device(): pl.pallas_call(kernel, out_shape=jax.ShapeDtypeStruct((rows, columns), BF...  156 us

profile of v4, /device:TPU:1, one launch (start us, length us, event | category | flops | bytes accessed | tf_op | source)
XLA Modules:
  0.0 157.9 jit_solution(14803222086962871458)
XLA Ops:
  0.0 156.2 %shard_map.64 = bf16[768,256]{1,0:T(8,128)(2,1)} custom-call(bf16[768,1024]{1,0:T(8,128)(2,1)} %samples.1, bf16[1024,256]{1,0:T(8,128)(2,1)} %gate.1, s32[2,768]{1,0:T(2,128)} %bitcast.3, s32[768]{0:T(1024)} %mask.1, bf16[4,4,256,1024]{3,2,1,0:T(8,128)(2,1)} %bitcast.2, bf16[1,1024,1024]{2,1,0:T(8,128)(2,1)} %down.1), custom_call_target="tpu_custom_call" | custom-call | tf_op jit(solution)/shard_map/pallas_call | solution.py:541
  156.2 1.8 %copy.8 = bf16[768,256]{1,0:T(8,128)(2,1)} copy(bf16[768,256]{1,0:T(8,128)(2,1)} %shard_map.64) | data formatting | bytes 786432

commit v5 on v4

--- a/solution.py
+++ b/solution.py
@@ -53,18 +53,19 @@
     peers = Y * C * X
 
     def to_plane(visit):
-        def one(i, k):
-            dc, dx = k % C, k // C
+        order = [(dx, dc) for dx in (2, 1, 3, 0) for dc in (1, 0)]
+
+        def one(i, dx, dc):
             y2, c2, x2 = lax.rem(y + dx + i, Y), lax.rem(c + dc, C), lax.rem(x + dx, X)
             visit(y2, c2, x2, ((y2 * Z + z) * C + c2, x2))
 
         def some(i, carry):
-            for k in range(C * X):
-                one(i, k)
+            for dx, dc in order:
+                one(i, dx, dc)
             return carry
 
-        for k in range(1, C * X):
-            one(0, k)
+        for dx, dc in order[:-1]:
+            one(0, dx, dc)
         lax.fori_loop(1, Y, some, 0)
 
     mine = (y * C + c) * X + x
@@ -310,14 +311,15 @@
     def back_copy(d):
         return remote(zs.at[d], zr.at[d], zsend.at[0], zrecv.at[d], at_z(-d))
 
-    def send_back(g, sources):
+    def sort_back(g, sources):
         n = width[g]
         q, i = iota((2 * half, peers * n), 0), iota((2 * half, peers * n), 1)
         base = q + div(q, CAP) * (n - CAP)
         got = rb[g][...].reshape(peers * n, rb[g].shape[2])
         for a, d in enumerate(sources):
             zs[d] = jnp.dot(as_mask(i == base + a * CAP), got, **EXACT).astype(BF16)
-            back_copy(d).start()
+            if g > 2:
+                back_copy(d).start()
 
     def add_up(plane, n, values, fresh=False):
         slots = target((1, values.shape[0]), 1, n, 0, plane)
@@ -435,7 +437,7 @@
     expert(1)
     second_hop(1)
     back_in_plane(1)
-    send_back(1, (1, Z - 1))
+    sort_back(1, (1, Z - 1))
     second_hop(2)
     second_hop(3)
     for a in range(2):
@@ -448,26 +450,27 @@
     third_hop(0)
     expert(2)
     third_hop(1)
-    gather_back(1)
     partly(3, 0)
     third_hop(2)
+    back_in_plane(2)
+    sort_back(2, (2, Z - 2))
+    third_hop(3)
+    for d in near_z:
+        back_copy(d).start()
     partly(3, 1)
-    back_in_plane(2)
-    third_hop(3)
-    send_back(2, (2, Z - 2))
+    fourth_hop(0)
     partly(3, 2)
-    fourth_hop(0)
     finish(3)
     fourth_hop(1)
     partly(4, 0)
     partly(4, 1)
     back_in_plane(3)
-    send_back(3, (3, Z - 3))
+    sort_back(3, (3, Z - 3))
     partly(4, 2)
     finish(4)
     back_in_plane(4)
-    send_back(4, (4,))
-    for d in (7, 2, 6, 3, 5):
+    sort_back(4, (4,))
+    for d in (1, 7, 2, 6, 3, 5):
         gather_back(d)
 
     block = fac.at[pl.ds(0, X - 1)]

time: 159 us -> 154 us (0.969)
  Pallas kernels: 156 us -> 152 us
    pallas_call x1, Pallas kernels: 156 us -> 152 us  [per_device(): pl.pallas_call(kernel, out_shape=jax.ShapeDtypeStruct((rows, columns), BF...]
where the time goes in v5:
time: 154 us
  Pallas kernels  152 us (99%)
  local copies, waits for them, and re-layouts  1.77 us (1%)
    pallas_call x1, Pallas kernels, per_device(): pl.pallas_call(kernel, out_shape=jax.ShapeDtypeStruct((rows, columns), BF...  152 us

profile of v5, /device:TPU:1, one launch (start us, length us, event | category | flops | bytes accessed | tf_op | source)
XLA Modules:
  0.0 154.2 jit_solution(13174018401682927633)
XLA Ops:
  0.0 152.4 %shard_map.64 = bf16[768,256]{1,0:T(8,128)(2,1)} custom-call(bf16[768,1024]{1,0:T(8,128)(2,1)} %samples.1, bf16[1024,256]{1,0:T(8,128)(2,1)} %gate.1, s32[2,768]{1,0:T(2,128)} %bitcast.3, s32[768]{0:T(1024)} %mask.1, bf16[4,4,256,1024]{3,2,1,0:T(8,128)(2,1)} %bitcast.2, bf16[1,1024,1024]{2,1,0:T(8,128)(2,1)} %down.1), custom_call_target="tpu_custom_call" | custom-call | tf_op jit(solution)/shard_map/pallas_call | solution.py:544
  152.5 1.8 %copy.8 = bf16[768,256]{1,0:T(8,128)(2,1)} copy(bf16[768,256]{1,0:T(8,128)(2,1)} %shard_map.64) | data formatting | bytes 786432

commit v6 on v5

--- a/solution.py
+++ b/solution.py
@@ -29,7 +29,7 @@
     sv, gv, w1, w2, near, hop, far, last,
     sb0, sb1, sb2, sb3, sb4, xb0, xb1, xb2, xb3, xb4,
     ob0, ob1, ob2, ob3, ob4, rb0, rb1, rb2, rb3, rb4,
-    zs, zr, posb, rowb, pick, pickr, cols, lpart, lrecv, fac, act, acc, hid, apart,
+    zs, zr, posb, rowb, pick, pickr, cols, lpart, lrecv, fac, act, acc, hid, apart, done,
     wsem, ssem, known, hsend, hrecv, isend, irecv, rsend, rrecv, zsend, zrecv, msend, mrecv,
 ):
     sb, xb = (sb0, sb1, sb2, sb3, sb4), (xb0, xb1, xb2, xb3, xb4)
@@ -490,8 +490,15 @@
     remote(sent, sent, zsend.at[0], zrecv.at[1], at_z(1)).wait_send()
 
     back_copy(4).wait_recv()
-    final = [acc[k] + jnp.dot(pick[k, :, 2 * half : 4 * half], zr[4], **EXACT) for k in range(2)]
-    out[...] = (scale[:, 0:1] * final[0] + scale[:, 1:2] * final[1]).astype(out.dtype)
+    leave = []
+    for h in range(2):
+        part = slice(h * rows // 2, (h + 1) * rows // 2)
+        final = [acc[k, part] + jnp.dot(pick[k, part, 2 * half : 4 * half], zr[4], **EXACT) for k in range(2)]
+        done[part] = (scale[part, 0:1] * final[0] + scale[part, 1:2] * final[1]).astype(out.dtype)
+        leave.append(local(done.at[part], out.at[part], ssem.at[h]))
+        leave[h].start()
+    for copy in leave:
+        copy.wait()
 
 
 def per_device(samples, gate_weight, expert_ids, pad_mask, up_weight, down_weight):
@@ -536,6 +543,7 @@
         pltpu.VMEM((2, rows, columns), F32),
         pltpu.VMEM((2, 4, Y * C * 24, hidden // 4), F32),
         pltpu.VMEM((Y * C * 16, depth // 4), BF16),
+        pltpu.VMEM((rows, columns), BF16),
     ]
     scratch += [
         dma((3,)), dma((nf,)), pltpu.SemaphoreType.REGULAR((7,)), dma((4,)), dma((2, 4, nf)), dma((5,)), dma((5, nf)),
@@ -545,7 +553,7 @@
         kernel,
         out_shape=jax.ShapeDtypeStruct((rows, columns), BF16),
         in_specs=[any_space, any_space, vmem, vmem, any_space, any_space],
-        out_specs=vmem,
+        out_specs=any_space,
         scratch_shapes=scratch,
         compiler_params=pltpu.CompilerParams(
             collective_id=0, has_side_effects=True, vmem_limit_bytes=67043328

time: 154 us -> 154 us (level)
  no operation moved by 1% of the time
where the time goes in v6:
time: 154 us
  Pallas kernels  152 us (99%)
  local copies, waits for them, and re-layouts  1.77 us (1%)
    pallas_call x1, Pallas kernels, per_device(): pl.pallas_call(kernel, out_shape=jax.ShapeDtypeStruct((rows, columns), BF...  152 us

profile of v6, /device:TPU:1, one launch (start us, length us, event | category | flops | bytes accessed | tf_op | source)
XLA Modules:
  0.0 154.2 jit_solution(10628029335019808476)
XLA Ops:
  0.0 152.4 %shard_map.64 = bf16[768,256]{1,0:T(8,128)(2,1)} custom-call(bf16[768,1024]{1,0:T(8,128)(2,1)} %samples.1, bf16[1024,256]{1,0:T(8,128)(2,1)} %gate.1, s32[2,768]{1,0:T(2,128)} %bitcast.3, s32[768]{0:T(1024)} %mask.1, bf16[4,4,256,1024]{3,2,1,0:T(8,128)(2,1)} %bitcast.2, bf16[1,1024,1024]{2,1,0:T(8,128)(2,1)} %down.1), custom_call_target="tpu_custom_call" | custom-call | tf_op jit(solution)/shard_map/pallas_call | solution.py:552
  152.4 1.8 %copy.8 = bf16[768,256]{1,0:T(8,128)(2,1)} copy(bf16[768,256]{1,0:T(8,128)(2,1)} %shard_map.64) | data formatting | bytes 786432

commit v7 on v5

--- a/solution.py
+++ b/solution.py
@@ -448,8 +448,8 @@
         p = (col[:, k : k + 1] * CAP + col[:, 2 + k : 3 + k]).astype(I32)
         pick[k, :, 2 * half : 4 * half] = as_mask(p == last_slots)
     third_hop(0)
+    third_hop(1)
     expert(2)
-    third_hop(1)
     partly(3, 0)
     third_hop(2)
     back_in_plane(2)

time: 154 us -> 155 us (level)
  no operation moved by 1% of the time
where the time goes in v7:
time: 155 us
  Pallas kernels  153 us (99%)
  local copies, waits for them, and re-layouts  1.77 us (1%)
    pallas_call x1, Pallas kernels, per_device(): pl.pallas_call(kernel, out_shape=jax.ShapeDtypeStruct((rows, columns), BF...  153 us

profile of v7, /device:TPU:1, one launch (start us, length us, event | category | flops | bytes accessed | tf_op | source)
XLA Modules:
  0.0 155.3 jit_solution(12995456304993876746)
XLA Ops:
  0.0 153.5 %shard_map.64 = bf16[768,256]{1,0:T(8,128)(2,1)} custom-call(bf16[768,1024]{1,0:T(8,128)(2,1)} %samples.1, bf16[1024,256]{1,0:T(8,128)(2,1)} %gate.1, s32[2,768]{1,0:T(2,128)} %bitcast.3, s32[768]{0:T(1024)} %mask.1, bf16[4,4,256,1024]{3,2,1,0:T(8,128)(2,1)} %bitcast.2, bf16[1,1024,1024]{2,1,0:T(8,128)(2,1)} %down.1), custom_call_target="tpu_custom_call" | custom-call | tf_op jit(solution)/shard_map/pallas_call | solution.py:544
  153.5 1.8 %copy.8 = bf16[768,256]{1,0:T(8,128)(2,1)} copy(bf16[768,256]{1,0:T(8,128)(2,1)} %shard_map.64) | data formatting | bytes 786432
